TPU v7x, 512 devices: a 4x2x32 block of a 4x8x32 slice. The times are simulated.
512 devices in a mesh: groups: 2 (over y), shell: 128 (over x, z), batch: 2 (over core).
Axes of the slice: x: 4, y: 2, z: 32, core: 2. Of those that a mesh axis runs over, the one named last changes fastest.
The devices are a block of a 4x8x32 slice.
Arguments:
- particles: bfloat16 [320, 16384], P(('groups', 'batch'), 'shell'), parts along dimension 0, may hold values from -5 to 5
- classes: bfloat16 [512, 16384], P('groups', 'shell'), parts along dimension 0, may hold values from -2.5 to 2.5
- ctf: float32 [16, 8192], P('groups', 'shell'), parts along dimension 0, may hold values from 0.1 to 1
- sigma2: float32 [128], P('groups'), parts along dimension 0, may hold values from 0.5 to 8
- shell_of: int32 [8192], P('shell'), may hold values from 0 to 63, as said below
- rot_table: int32 [48, 8192], P(None, 'shell'), may hold values from 0 to 8191, as said below
- ctf_group: int32 [320], P(('groups', 'batch')), parts along dimension 0, may hold values from 0 to 7
Outputs:
- class_sums: float32 [512, 16384], P('groups', 'shell'), parts along dimension 0
- class_weights: float32 [512, 8192], P('groups', 'shell'), parts along dimension 0
- log_evidence: float32 [320], P(('groups', 'batch')), parts along dimension 0
There are 2 independent parts, one for each index of `groups`. A program takes and returns all parts, laid end to end along the dimension named above; an argument that names none is the same for every part. Nothing has to cross between parts.
Inputs may be any that keep to these rules, and one draw needn't show every extreme that they name: shell_of never falls along the coefficients; its first entry is 0 and its last 63. `rot_table`: for each rotation, each aligned block of 64 coefficients is mapped onto itself one to one; rotation 0 maps every coefficient to itself.
All inputs are finite; a program needn't handle non-finite values.
Results may differ from a plain program's by a relative error of at most 0.0041.
Values may be sent and summed in bfloat16 or wider, within the bound.
A program may use at most 64 MiB of HBM per device.

v0:
```python
import jax
import jax.numpy as jnp
from jax import lax
from jax.sharding import Mesh
from jax.sharding import PartitionSpec as P

SHELL = ("shell_0", "shell_1")


def scatter_axes(shard, axes, dim):
    if not axes:
        return shard
    nearer = lax.psum_scatter(shard, axes[0], scatter_dimension=dim, tiled=True)
    return scatter_axes(nearer, axes[1:], dim)


def collected_together(shard, axis):
    leaves = jax.tree.leaves(shard)
    sequence = sorted(range(len(leaves)), key=lambda k: -leaves[k].size)
    width = (1, *leaves[sequence[0]].shape)[-1]
    lines = [
        jnp.pad(leaves[k].reshape(-1), (0, -leaves[k].size % width)).reshape(-1, width)
        for k in sequence
    ]
    both, at, found = (lax.all_gather(jnp.concatenate(lines), axis), 0, {})
    for k, line in zip(sequence, lines):
        section = both[:, at : at + len(line)].reshape(len(both), -1)
        found[k] = section[:, : leaves[k].size].reshape(-1, *leaves[k].shape)
        at += len(line)
    numbers = iter(range(len(leaves)))
    return jax.tree.map(lambda _: found[next(numbers)], shard)


def merged(shard, axis, combine):
    everything = collected_together(shard, axis)
    first = jax.tree.map(lambda part: part[0], everything)

    def turn(k, so_far):
        return combine(so_far, jax.tree.map(lambda part: part[k], everything))

    return lax.fori_loop(1, lax.axis_size(axis), turn, first)


def laid_out(tiles, dim):
    tiles = jnp.moveaxis(tiles, 0, dim)
    dims = tiles.shape
    return tiles.reshape(*dims[:dim], dims[dim] * dims[dim + 1], *dims[dim + 2 :])


def all_blocks(shard, axes, sequence):
    tiles = shard
    for k in sequence:
        tiles = lax.all_gather(tiles, axes[k])
    done = sequence[::-1]
    back = [done.index(k) for k in range(len(axes))]
    tiles = tiles.transpose(*back, *range(len(axes), tiles.ndim))
    return tiles.reshape(-1, *shard.shape)


def gathered_by_axis(shard, axes, sequence, dim):
    return laid_out(all_blocks(shard, axes, sequence), dim)


def sent_to_all(shard, axis):
    count = lax.axis_size(axis)
    return lax.all_to_all(
        jnp.broadcast_to(shard[None], (count, *shard.shape)), axis, 0, 0, tiled=True
    )


def of_everyone(shard, axis):
    everything = sent_to_all(shard, axis)
    return jnp.sum(everything, axis=0)


def packed_total(arrays, axis):
    ends = [0]
    for a in arrays:
        ends.append(ends[-1] + a.size)
    subtotal = of_everyone(jnp.concatenate([a.ravel() for a in arrays]), axis)
    return tuple((subtotal[b:e].reshape(a.shape) for a, b, e in zip(arrays, ends, ends[1:])))


def combine(earlier, later):
    larger = jnp.maximum(earlier[0], later[0])
    summed = earlier[1] * jnp.exp(earlier[0] - larger) + later[1] * jnp.exp(later[0] - larger)
    return (larger, summed)


def body(particles, classes, ctf, sigma2, shell_of, rot_table, ctf_group):
    highest = lax.Precision.HIGHEST
    coef_width = shell_of.shape[0]
    class_count = classes.shape[0]
    rotations = rot_table.shape[0]
    levels = sigma2.shape[0]
    group_count = ctf.shape[0]
    offset = lax.axis_index(SHELL) * coef_width
    local_table = rot_table - offset
    pick_shell = (shell_of[:, None] == jnp.arange(levels, dtype=jnp.int32)[None, :]).astype(
        jnp.float32
    )
    weight = 1.0 / jnp.dot(
        pick_shell, sigma2, precision=highest, preferred_element_type=jnp.float32
    )
    pick_group = (ctf_group[:, None] == jnp.arange(group_count, dtype=jnp.int32)[None, :]).astype(
        jnp.float32
    )
    ctf_part = jnp.dot(pick_group, ctf, precision=highest, preferred_element_type=jnp.float32)
    values = particles.astype(jnp.float32)
    real_part = values[:, :coef_width]
    imag_part = values[:, coef_width:]
    weighted_ctf = weight[None, :] * ctf_part
    weighted = jnp.concatenate([weighted_ctf * real_part, weighted_ctf * imag_part], axis=1).astype(
        jnp.bfloat16
    )
    ctf_power = weight[None, :] * ctf * ctf
    sources = jnp.concatenate(
        [ctf_part * real_part, ctf_part * imag_part, ctf_part * ctf_part], axis=1
    ).astype(jnp.bfloat16)
    class_view = classes.reshape(class_count, 2, coef_width)
    rotated = jnp.take(class_view, local_table, axis=2)
    rotated = jnp.transpose(rotated, (0, 2, 1, 3)).reshape(class_count * rotations, 2 * coef_width)
    cross_terms = lax.dot_general(
        weighted, rotated, (((1,), (1,)), ((), ())), preferred_element_type=jnp.float32
    )
    rot_float = rotated.astype(jnp.float32)
    class_power = rot_float[:, :coef_width] ** 2 + rot_float[:, coef_width:] ** 2
    penalty = lax.dot_general(
        ctf_power,
        class_power,
        (((1,), (1,)), ((), ())),
        precision=highest,
        preferred_element_type=jnp.float32,
    )
    score_share = scatter_axes(
        cross_terms
        - 0.5 * jnp.dot(pick_group, penalty, precision=highest, preferred_element_type=jnp.float32),
        SHELL,
        1,
    )
    peak = jnp.max(score_share, axis=1)
    exp_total = jnp.sum(jnp.exp(score_share - peak[:, None]), axis=1)
    peak, exp_total = merged((peak, exp_total), SHELL, combine)
    log_evidence = peak + jnp.log(exp_total)
    post_share = jnp.exp(score_share - log_evidence[:, None]).astype(jnp.bfloat16)
    frames = lax.dot_general(
        gathered_by_axis(post_share, SHELL, (0, 1), 1),
        sources,
        (((0,), (0,)), ((), ())),
        preferred_element_type=jnp.float32,
    )
    frames = frames.reshape(class_count, rotations, 3, coef_width)
    placing = (
        local_table[:, :, None] == jnp.arange(coef_width, dtype=jnp.int32)[None, None, :]
    ).astype(jnp.float32)
    unrotated = jnp.einsum(
        "krqc,rcd->kqd", frames, placing, precision=highest, preferred_element_type=jnp.float32
    )
    sums_part = unrotated[:, 0:2].reshape(class_count, 2 * coef_width)
    weights_part = unrotated[:, 2]
    class_sums, class_weights = packed_total((sums_part, weights_part), "batch")
    return (class_sums, class_weights, log_evidence)


def solution(mesh):
    split = Mesh(
        mesh.devices.reshape(mesh.shape["groups"], 4, 32, mesh.shape["batch"]),
        ("groups", "shell_0", "shell_1", "batch"),
    )
    placed = (
        P(("groups", "batch"), SHELL),
        P("groups", SHELL),
        P("groups", SHELL),
        P("groups"),
        P(SHELL),
        P(None, SHELL),
        P(("groups", "batch")),
    )
    return jax.shard_map(
        body,
        mesh=split,
        in_specs=placed,
        out_specs=(P("groups", SHELL), P("groups", SHELL), P(("groups", "batch"))),
        check_vma=False,
    )
```

profile of v0, /device:TPU:33, one launch (start us, length us, event | category | flops | bytes accessed | tf_op | source)
XLA Modules:
  0.0 627.4 jit_solution(13757328853262654818)
XLA Ops:
  7.3 0.8 copy.57
  8.1 0.9 copy.58
  9.1 0.8 compare_and_fusion
  10.0 11.7 %gather_fusion = bf16[3072,256,2]{1,2,0:T(2,128)(2,1)S(1)} fusion(bf16[256,2,64]{0,1,2:T(2,128)(2,1)S(1)} %copy.59, s32[3072]{0:T(1024)S(1)} %broadcast_clamp_fusion), kind=kCustom, calls=%fused_computation | custom fusion | bytes 6303744 | tf_op jit(solution)/shard_map/jit(_take)/gather | solution.py:121
  21.7 0.5 copy.60
  22.1 0.6 select_bitcast_fusion
  22.7 10.8 %copy.61 = bf16[256,48,2,64]{3,2,1,0:T(2,128)(2,1)} copy(bf16[256,48,2,64]{0,3,1,2:T(8,128)(2,1)S(1)} %select_bitcast_fusion) | data formatting | bytes 6291456 | tf_op jit(solution)/shard_map/jit(_take)/select_n | solution.py:121
  33.5 9.8 %reshape.73 = bf16[12288,128]{1,0:T(8,128)(2,1)S(1)} reshape(bf16[256,48,2,64]{3,2,1,0:T(2,128)(2,1)} %copy.61) | data formatting | bytes 6291456 | tf_op jit(solution)/shard_map/reshape | solution.py:122
  43.4 0.5 convert_element_type.7
  44.2 5.9 fusion.4
  50.3 1.2 fusion.17
  51.6 3.9 fusion.2
  55.8 86.2 %reduce-scatter.5.cloned.1.call-done = f32[80,3072]{1,0:T(8,128)} async-done(((f32[80,12288]{1,0:T(8,128)}), f32[80,3072]{1,0:T(8,128)}) %reduce-scatter.5.cloned.1.call-update) | async-done | bytes 983056 | tf_op jit(solution)/shard_map/reduce_scatter | solution.py:13
  142.0 2.8 copy.72
  145.0 113.6 %reduce-scatter.7.cloned.1.call-done = f32[96,80]{1,0:T(8,128)} async-done(((f32[3072,80]{1,0:T(8,128)}), f32[96,80]{1,0:T(8,128)}) %reduce-scatter.7.cloned.1.call-update) | async-done | bytes 30736
  258.6 0.9 copy.73
  259.5 0.8 bitcast_reduce_fusion
  260.5 123.7 %all-gather.3 = f32[128,2,80]{2,1,0:T(2,128)S(1)} all-gather(f32[1,2,80]{2,1,0:T(2,128)S(1)} %maximum_bitcast_fusion), channel_id=2, replica_groups=mesh['groups'=2,'shell_0'=4,'shell_1'=32,'batch'=2] {'shell_0','shell_1'}, dimensions={0}, use_global_device_ids=true | all-gather | bytes 82560 | tf_op jit(solution)/shard_map/all_gather | solution.py:25
  384.4 5.7 while.17
  390.2 9.8 %all-gather.1 = bf16[320,96]{1,0:T(8,128)(2,1)} all-gather(bf16[80,96]{1,0:T(8,128)(2,1)S(1)} %exponential_convert_fusion), channel_id=3, replica_groups=mesh['groups'=2,'shell_0'=4,'shell_1'=32,'batch'=2] {'shell_0'}, dimensions={0}, use_global_device_ids=true | all-gather | bytes 76800 | tf_op jit(solution)/shard_map/all_gather | solution.py:53
  400.1 172.5 %all-gather.6.cloned.1.call-done = bf16[128,80,96]{2,1,0:T(8,128)(2,1)} async-done(((bf16[4,80,96]{2,1,0:T(8,128)(2,1)}), bf16[128,80,96]{2,1,0:T(8,128)(2,1)}) %all-gather.6.cloned.1.call-update) | async-done | bytes 1966096 | tf_op jit(solution)/shard_map/all_gather | solution.py:53
  572.6 1.9 copy.62
  574.6 0.7 copy.63
  575.3 4.7 reshape.79
  580.0 3.3 copy.64
  583.2 3.1 copy.65
  586.3 2.9 fusion.6
  589.2 4.0 fusion.11
  594.1 24.8 %all_to_all.6 = f32[2,1,49152]{2,1,0:T(1,128)S(1)} all-to-all(f32[2,1,49152]{2,1,0:T(1,128)S(1)} %broadcast_in_dim.17), channel_id=1, replica_groups=mesh['groups'=2,'shell_0'=4,'shell_1'=32,'batch'=2] {'batch'}, dimensions={0} | all-to-all | bytes 786432 | tf_op jit(solution)/shard_map/all_to_all | solution.py:66
  618.9 0.6 reduce_sum.19
  619.4 0.7 slice_bitcast_fusion
  620.2 0.7 copy.69
  (167 shorter events, 6.0 us)
Async XLA Ops:
  7.2 36.6 %copy-start = (f32[64]{0:T(128)S(1)}, f32[64]{0:T(128)}, u32[]{:S(2)}) copy-start(f32[64]{0:T(128)} %param.12) | copy-start | bytes 772
  7.2 134.8 %reduce-scatter.5.cloned.1.call-start = ((), (), s32[]{:S(2)}) async-start(), calls=%async_computation.3 | async-start | bytes 4915200 | tf_op jit(solution)/shard_map/reduce_scatter | solution.py:13
  43.3 0.7 copy-start.4
  43.3 0.8 copy-start.3
  44.0 6.1 copy-start.1
  55.6 203.0 %reduce-scatter.7.cloned.1.call-start = ((), (), s32[]{:S(2)}) async-start(), calls=%async_computation.5 | async-start | bytes 1622016
  144.9 427.7 %all-gather.6.cloned.1.call-start = ((), (), s32[]{:S(2)}) async-start(), calls=%async_computation.4 | async-start | bytes 2703360 | tf_op jit(solution)/shard_map/all_gather | solution.py:53
  390.1 185.1 %copy-start.2 = (f32[80]{0:T(128)}, f32[80]{0:T(128)S(1)}, u32[]{:S(2)}) copy-start(f32[80]{0:T(128)S(1)} %log_add_fusion) | copy-start | bytes 964
Sparse Core Ops, SparseCore 0:
  55.7 86.2 reduce-scatter.4
  145.1 113.5 reduce-scatter.6
  400.2 172.3 all-gather.5
where the time goes:
time: 628 us; the launch traced here: 627 us
  waiting for transfers between devices  372 us (59%)
  blocking collectives  158 us (25%)
  local copies, waits for them, and re-layouts  54.5 us (9%)
  matrix products  18.5 us (3%)
  between operations  14.1 us (2%)
  other arithmetic  6.99 us (1%)
    all_gather x1, waiting for transfers between devices, all_blocks(): tiles = lax.all_gather(tiles, axes[k])  173 us
    all_gather x1, blocking collectives, collected_together(): both, at, found = (lax.all_gather(jnp.concatenate(lines), axis), 0, {})  124 us
    unnamed x4, waiting for transfers between devices  114 us
    reduce_scatter x1, waiting for transfers between devices, scatter_axes(): nearer = lax.psum_scatter(shard, axes[0], scatter_dimension=dim, tiled=True)  86.2 us
    all_to_all x1, blocking collectives, sent_to_all(): lax.all_to_all(jnp.broadcast_to(shard[None], (count, *shard.shape)), axis...  24.8 us
  transfers between devices with their start and end apart: 3, of which 3 were waited for; matrix products, arithmetic and copies ran while one was open for 0% of the time, Pallas kernels for 0%

commit v1 on v0

v1 whole, which is shorter than its diff:
```python
import functools

import jax
import jax.numpy as jnp
from jax import lax
from jax.experimental import pallas as pl
from jax.experimental.pallas import tpu as pltpu
from jax.sharding import Mesh
from jax.sharding import PartitionSpec as P

MESH = pl.DeviceIdType.MESH
ROW = 4
SIDE = 4
NP = ROW * SIDE
OWNERS = 4
LANES = 128
F32 = jnp.float32
BF16 = jnp.bfloat16
NT = (((1,), (1,)), ((), ()))
AXES = ("groups", "x", "z", "batch")


def lane(shape):
    return lax.broadcasted_iota(jnp.int32, shape, 1)


def compact(w):
    free = lane((8, LANES)) >= 80
    kept = []
    for r in range(0, w.shape[0], 48):
        a, b = w[r + 32 : r + 40], w[r + 40 : r + 48]
        kept += [
            jnp.where(free, pltpu.roll(a, 80, 1), w[r : r + 8]),
            jnp.where(free, pltpu.roll(a, 32, 1), w[r + 8 : r + 16]),
            jnp.where(free, pltpu.roll(b, 80, 1), w[r + 16 : r + 24]),
            jnp.where(free, pltpu.roll(b, 32, 1), w[r + 24 : r + 32]),
        ]
    return jnp.concatenate(kept, axis=0)


def expand(w):
    first = lane((8, LANES)) < 48
    whole = []
    for r in range(0, w.shape[0], 32):
        part = w[r : r + 32]
        whole += [
            part,
            jnp.where(first, pltpu.roll(part[0:8], 48, 1), pltpu.roll(part[8:16], 96, 1)),
            jnp.where(first, pltpu.roll(part[16:24], 48, 1), pltpu.roll(part[24:32], 96, 1)),
        ]
    return jnp.concatenate(whole, axis=0)


def spread(row):
    free = lane((1, LANES)) >= 80
    return jnp.where(free, pltpu.roll(row, 80, 1), row), jnp.where(free, pltpu.roll(row, 32, 1), row)


def tiles(even, odd, rows):
    e = jnp.broadcast_to(even, (8, LANES))
    o = jnp.broadcast_to(odd, (8, LANES))
    return jnp.concatenate([e, o] * (rows // 16), axis=0)


def over_rows(values, combine, reduce):
    split = [values[r : r + 8] for r in range(0, values.shape[0], 8)]
    even = reduce(functools.reduce(combine, split[0::2]), axis=0, keepdims=True)
    odd = reduce(functools.reduce(combine, split[1::2]), axis=0, keepdims=True)
    first = lane((1, LANES)) < 48
    moved = jnp.where(first, pltpu.roll(even, 48, 1), pltpu.roll(odd, 96, 1))
    return combine(combine(even, odd), moved)


def kernel(
    nz,
    part_hbm,
    cls_hbm,
    ctf_hbm,
    sig_hbm,
    sh_hbm,
    tab_hbm,
    grp_hbm,
    mine_ref,
    other_ref,
    ev_ref,
    cls_ref,
    ctf_ref,
    sig_ref,
    sh_ref,
    tab_ref,
    grp_ref,
    bundle,
    cls_z,
    cls_all,
    place,
    w_all,
    src_all,
    left,
    rot_all,
    score,
    rs_send,
    rs_scale,
    rs_recv,
    rs_rscale,
    ag_send,
    top_send,
    ag_recv,
    top_recv,
    lse_own,
    lse_all,
    post,
    frame,
    out_send,
    sizes,
    in_sem,
    g_ssem,
    z_rsem,
    x_rsem,
    rs_ssem,
    rs_rsem,
    ag_ssem,
    ag_rsem,
    top_rsem,
    lse_ssem,
    lse_rsem,
    o_ssem,
    o_rsem,
    c_ssem,
    c_rsem,
    owner_in,
):
    nb = nz // SIDE
    count, coef = part_hbm.shape[0], ctf_ref.shape[1]
    kb = cls_all.shape[1]
    half = tab_ref.shape[0] // 2
    rows = half * kb // OWNERS
    group = lax.axis_index("groups")
    x = lax.axis_index("x")
    z = lax.axis_index("z")
    core = lax.axis_index("batch")
    zb, zi = z // SIDE, lax.rem(z, SIDE)
    me = zi * ROW + x
    owner = jnp.where(
        jnp.logical_and(zb >= 1, zb < 3), zb - 1, jnp.where(jnp.logical_and(zb >= nb - 3, zb < nb - 1), zb - nb + 5, OWNERS)
    )

    def home(o):
        return jnp.where(o < 2, o + 1, o + nb - 5)

    def turn_in(b):
        return jnp.where(b == 0, nb - 2, jnp.where(b == nb - 1, nb - 1, b - 1))

    my_turn = turn_in(zb)

    def at(x_, z_):
        return (group, x_, z_, core)

    def mate(k):
        i = lax.rem(me + k, NP)
        return i, at(lax.rem(i, ROW), zb * SIDE + i // ROW)

    def far(b):
        return at(x, b * SIDE + zi)

    partner = (group, x, z, 1 - core)

    def remote(src, dst, ssem, rsem, device):
        return pltpu.make_async_remote_copy(
            src_ref=src, dst_ref=dst, send_sem=ssem, recv_sem=rsem, device_id=device, device_id_type=MESH
        )

    def drain(semaphore, size):
        whole = sizes.at[0:size]
        remote(whole, whole, semaphore, semaphore, partner).wait_recv()

    def each(lower, upper, step):
        def turn(k, _):
            step(k)
            return 0

        lax.fori_loop(lower, upper, turn, 0)

    def tell(semaphore, device):
        pl.semaphore_signal(semaphore, inc=1, device_id=device, device_id_type=MESH)

    def rows_of(i, n):
        return pl.ds(pl.multiple_of(i * n, n), n)

    given = (ctf_hbm, sig_hbm, sh_hbm, tab_hbm, part_hbm, cls_hbm.at[rows_of(zi, ROW * kb)], cls_hbm, grp_hbm)
    taken = (ctf_ref, sig_ref, sh_ref, tab_ref, bundle.at[me, 0:count], cls_z.at[zi], cls_ref, grp_ref)
    loads = [pltpu.make_async_copy(a, b, in_sem.at[k]) for k, (a, b) in enumerate(zip(given, taken))]
    for load in loads:
        load.start()

    barrier = pltpu.get_barrier_semaphore()
    each(1, NP, lambda k: tell(barrier, mate(k)[1]))
    tell(barrier, partner)

    def greet_later(b):
        @pl.when(turn_in(b) > my_turn)
        def _():
            tell(barrier, far(b))

    each(0, nb, greet_later)
    for load in loads[:4]:
        load.wait()

    levels = sig_ref.shape[1]
    pick = (lax.broadcasted_iota(jnp.int32, (levels, coef), 0) == sh_ref[...]).astype(F32)
    noise = jnp.dot(
        jnp.broadcast_to(sig_ref[...], (8, levels)), pick, precision=lax.Precision.HIGHEST, preferred_element_type=F32
    )
    ctf = ctf_ref[...]
    par = jnp.concatenate([ctf, (1.0 / noise[0:1]) * ctf], axis=1)
    par_high = par.astype(BF16).astype(F32)
    par_mid = (par - par_high).astype(BF16).astype(F32)
    offset = (x * nz + z) * coef
    table = (tab_ref[...] - offset).astype(F32)
    table = jnp.concatenate([table[:half], table[half:]], axis=1)
    bundle[me, count:] = jnp.concatenate([table, par_high, par_mid, (par - par_high) - par_mid], axis=0).astype(BF16)
    for load in loads[4:]:
        load.wait()
    with jax.named_scope("barrier"):
        pl.semaphore_wait(barrier, NP + my_turn)

    def down(k):
        i = lax.rem(zi + k, SIDE)
        device = at(x, zb * SIDE + i)
        remote(bundle.at[me], bundle.at[me], g_ssem, z_rsem.at[zi], device).start()
        remote(cls_ref.at[rows_of(i, ROW * kb)], cls_z.at[zi], g_ssem, z_rsem.at[zi], device).start()

    def across(i):
        b = i * ROW + x
        for k in range(1, ROW):
            to = lax.rem(x + k, ROW)
            device = at(to, z)
            remote(bundle.at[b], bundle.at[b], g_ssem, x_rsem.at[b], device).start()
            remote(cls_z.at[i, rows_of(to, kb)], cls_all.at[b], g_ssem, x_rsem.at[b], device).start()

    bundle_size = bundle.shape[1] // 2
    each(1, SIDE, down)
    across(zi)

    @pl.when(owner < OWNERS)
    def _():
        def tell_earlier(b):
            @pl.when(turn_in(b) < my_turn)
            def _():
                tell(owner_in.at[owner], far(b))

        each(0, nb, tell_earlier)

    with jax.named_scope("zeros"):
        w_all[...] = jnp.zeros_like(w_all)
        src_all[...] = jnp.zeros_like(src_all)
        left[...] = jnp.zeros_like(left)
    score[...] = jnp.zeros_like(score)
    cls_all[me] = cls_z[zi, rows_of(x, kb), :]
    member = jnp.broadcast_to(grp_ref[...].astype(F32), (LANES, count)).T
    low = lane((count, LANES)) < coef
    low_kb = lane((kb, LANES)) < coef

    def pass_on(i):
        @pl.when(i != zi)
        def _():
            with jax.named_scope("came_down"):
                drain(z_rsem.at[i], bundle_size + ROW * kb // 2)
            across(i)
            cls_all[i * ROW + x] = cls_z[i, rows_of(x, kb), :]

    def amplitudes(tail):
        par = tail[half : half + 8] + tail[half + 8 : half + 16] + tail[half + 16 : half + 24]
        sel = jnp.broadcast_to(par[0:1], (count, LANES))
        for g in range(1, par.shape[0]):
            sel = jnp.where(member == g, par[g : g + 1], sel)
        other = pltpu.roll(sel, coef, 1)
        return jnp.where(low, sel, other), jnp.where(low, other, sel)

    def turned_over(a):
        return jnp.concatenate([a, jnp.zeros((LANES - count, LANES), F32)], axis=0).astype(BF16).T

    def prepare(g, i):
        b = g * 4 + i
        landing = bundle[b, count:].astype(F32)
        amp, wamp = amplitudes(landing)
        weighted = turned_over(wamp * bundle[b, 0:count].astype(F32))
        pen = -0.5 * (wamp * amp)
        pen_hi = pen.astype(BF16).astype(F32)
        pen = turned_over(jnp.where(low, pen_hi, pen - pen_hi))
        for s in range(2):
            lanes = slice(s * LANES, (s + 1) * LANES)
            for k, piece in enumerate((weighted[:coef], weighted[coef:], pen[:coef], pen[:coef], pen[coef:])):
                top = (5 * i + k) * LANES + s * coef
                w_all[g, top : top + coef, lanes] = piece
        index = lax.broadcasted_iota(jnp.int32, (coef, LANES), 0).astype(F32).astype(BF16)
        ones, zeros = jnp.ones((coef, LANES), BF16), jnp.zeros((coef, LANES), BF16)
        for j in range(half):
            row = jnp.broadcast_to(landing[j : j + 1], (16, LANES)).astype(BF16)
            row = jnp.concatenate([row] * (coef // 16), axis=0)
            place[rows_of(b, coef), j * LANES : (j + 1) * LANES] = jnp.where(index == row, ones, zeros)

    def prepare_sources(b):
        amp, _ = amplitudes(bundle[b, count:].astype(F32))
        source = amp * bundle[b, 0:count].astype(F32)
        source_turned = pltpu.roll(source, coef, 1)
        power = amp * amp
        for s in range(2):
            top = s * LANES

            def keep(lower, upper):
                return (jnp.where(low, lower, 0.0) if s == 0 else jnp.where(low, 0.0, upper)).astype(BF16)

            src_all[b, top : top + count, 0:128] = keep(source, source_turned)
            src_all[b, top : top + count, 128:256] = keep(source_turned, source)
            src_all[b, top : top + count, 256:384] = keep(power, power)

    def rotate(g):
        for i in range(4):
            image = cls_all[g * 4 + i].astype(F32)
            turned = pltpu.roll(image, coef, 1)
            if i % 2 == 0:
                re, im = jnp.where(low_kb, image, 0.0), jnp.where(low_kb, turned, 0.0)
            else:
                re, im = jnp.where(low_kb, 0.0, turned), jnp.where(low_kb, 0.0, image)
            top = (i // 2) * LANES
            left[g, 2 * i * kb : (2 * i + 1) * kb, top : top + LANES] = re.astype(BF16)
            left[g, (2 * i + 1) * kb : (2 * i + 2) * kb, top : top + LANES] = im.astype(BF16)
        lhs = left[g]
        for jj in range(half // 2):
            turned = jnp.dot(
                lhs, place[rows_of(g, 4 * coef), jj * 256 : (jj + 1) * 256], preferred_element_type=F32
            )
            for i in range(4):
                for t in range(2):
                    j = jj * 2 + t
                    re = turned[2 * i * kb : (2 * i + 1) * kb, t * LANES : (t + 1) * LANES]
                    im = turned[(2 * i + 1) * kb : (2 * i + 2) * kb, t * LANES : (t + 1) * LANES]
                    power = re * re + im * im
                    power_hi = power.astype(BF16)
                    power_lo = (power - power_hi.astype(F32)).astype(BF16)
                    to = slice(j * kb, (j + 1) * kb)
                    pieces = re.astype(BF16), im.astype(BF16), power_hi, power_lo, power_hi
                    for k, piece in enumerate(pieces):
                        at_lane = (5 * i + k) * LANES
                        rot_all[g, to, at_lane : at_lane + LANES] = piece

    def score_row(g):
        with jax.named_scope("arrive"):
            each(1, ROW, lambda k: drain(x_rsem.at[g * ROW + lax.rem(x + k, ROW)], bundle_size + kb // 2))
        with jax.named_scope("prepare"):
            for i in range(ROW):
                prepare(g, i)
        with jax.named_scope("scores"):
            rotate(g)
            score[...] += jnp.dot(rot_all[g], w_all[g], preferred_element_type=F32)

    each(0, SIDE - 1, pass_on)

    def turn_of(g):
        @pl.when(g == 1)
        def _():
            pass_on(SIDE - 1)

        score_row(g)

    each(0, SIDE, turn_of)

    def share(o):
        return score[rows_of(o, rows), :]

    share_size = rs_send.shape[1] + rs_scale.shape[1]
    for o in (1, 2, 0, 3):

        @pl.when(owner != o)
        def _():
            piece = share(o)
            one, two = piece[:, :LANES], piece[:, LANES:]
            most = jnp.max(jnp.maximum(one, two), axis=0, keepdims=True)
            least = jnp.min(jnp.minimum(one, two), axis=0, keepdims=True)
            middle = 0.5 * (most + least)
            reach = jnp.maximum(0.5 * (most - least), 1e-30)
            fit = 32767.0 / reach
            one = jnp.round((one - middle) * fit).astype(jnp.int32)
            two = jnp.round((two - middle) * fit).astype(jnp.int32)
            rs_send[o] = compact((one & 0xFFFF) | (two << 16))
            rs_scale[o] = jnp.concatenate([*spread(reach * (1.0 / 32767.0)), *spread(middle)], axis=0)

            @pl.when(turn_in(home(o)) > my_turn)
            def _():
                with jax.named_scope("owner_in"):
                    pl.semaphore_wait(owner_in.at[o], 1)

            with jax.named_scope("share_go"):
                remote(rs_send.at[o], rs_recv.at[zb], rs_ssem, rs_rsem.at[zb], far(home(o))).start()
                remote(rs_scale.at[o], rs_rscale.at[zb], rs_ssem, rs_rsem.at[zb], far(home(o))).start()

    with jax.named_scope("sources"):
        each(0, NP, prepare_sources)

    @pl.when(owner < OWNERS)
    def _():
        own = share(owner)
        total = compact(own[:, :LANES]), compact(own[:, LANES:])

        def add_share(k, so_far):
            b = jnp.where(k < zb, k, k + 1)
            with jax.named_scope("share_in"):
                drain(rs_rsem.at[b], share_size)
            word = rs_recv[b]
            step = tiles(rs_rscale[b, 0:1], rs_rscale[b, 1:2], word.shape[0])
            middle = tiles(rs_rscale[b, 2:3], rs_rscale[b, 3:4], word.shape[0])
            return (
                so_far[0] + (((word << 16) >> 16).astype(F32) * step + middle),
                so_far[1] + ((word >> 16).astype(F32) * step + middle),
            )

        total_one, total_two = lax.fori_loop(0, nb - 1, add_share, total)
        peak = over_rows(jnp.maximum(total_one, total_two), jnp.maximum, jnp.max)
        shift = tiles(*spread(peak), total_one.shape[0])
        exp_one, exp_two = jnp.exp(total_one - shift), jnp.exp(total_two - shift)
        evidence = peak + jnp.log(over_rows(exp_one + exp_two, jnp.add, jnp.sum))
        top_send[...] = jnp.concatenate([peak, evidence], axis=0)

        def send_top(b):
            @pl.when(b != zb)
            def _():
                remote(top_send, top_recv.at[owner], ag_ssem, top_rsem.at[owner], far(b)).start()

        each(0, nb, send_top)
        one = (exp_one * 65535.0 + 0.5).astype(jnp.int32)
        two = (exp_two * 65535.0 + 0.5).astype(jnp.int32)
        ag_send[...] = (one & 0xFFFF) | (two << 16)

        def send_post(b):
            @pl.when(b != zb)
            def _():
                remote(ag_send, ag_recv.at[owner], ag_ssem, ag_rsem.at[owner], far(b)).start()

        each(0, nb, send_post)
        ag_recv[owner] = ag_send[...]
        top_recv[owner] = top_send[...]

    def take_top(o):
        @pl.when(o != owner)
        def _():
            with jax.named_scope("top_in"):
                drain(top_rsem.at[o], top_send.shape[0])

    each(0, OWNERS, take_top)

    def merged(parts):
        most = functools.reduce(jnp.maximum, parts)
        return most + jnp.log(functools.reduce(jnp.add, [jnp.exp(e - most) for e in parts]))

    evidence = merged([top_recv[o, 1:2] for o in range(OWNERS)])
    lse_own[...] = evidence
    each(1, NP, lambda k: remote(lse_own, lse_all.at[me], lse_ssem, lse_rsem, mate(k)[1]).start())
    lse_all[me] = evidence
    with jax.named_scope("lse_in"):
        drain(lse_rsem, NP - 1)
    everyone = lse_all[...]
    most = jnp.max(everyone, axis=0)
    evidence = most + jnp.log(jnp.sum(jnp.exp(everyone - most[None]), axis=0))
    ev_ref[...] = evidence
    used = lane((rows, LANES)) < count

    def take_post(o):
        @pl.when(o != owner)
        def _():
            with jax.named_scope("post_in"):
                drain(ag_rsem.at[o], ag_send.shape[0])

        word = expand(ag_recv[o])
        scale = jnp.exp(top_recv[o, 0:1] - evidence) * (1.0 / 65535.0)
        one = jnp.where(used, (word & 0xFFFF).astype(F32) * scale, 0.0)
        two = jnp.where(used, lax.shift_right_logical(word, 16).astype(F32) * scale, 0.0)
        post[rows_of(o, rows), 0:128] = one.astype(BF16)
        post[rows_of(o, rows), 128:256] = two.astype(BF16)

    each(0, OWNERS, take_post)

    def class_row(i):
        for k in range(ROW):
            frames = jnp.dot(post[...], src_all[i * ROW + k], preferred_element_type=F32)
            for j in range(half):
                for t in range(3):
                    frame[k, t * kb : (t + 1) * kb, j * LANES : (j + 1) * LANES] = frames[
                        j * kb : (j + 1) * kb, t * LANES : (t + 1) * LANES
                    ].astype(BF16)
        for k in range(ROW):
            turned = place[rows_of(i * ROW + k, coef), :]
            sums = lax.dot_general(frame[k], turned, NT, preferred_element_type=F32)
            weights = sums[2 * kb : 3 * kb]
            out_send[i * ROW + k] = jnp.concatenate(
                [
                    jnp.concatenate([sums[0:kb], sums[kb : 2 * kb]], axis=1),
                    jnp.concatenate([weights[: kb // 2], weights[kb // 2 :]], axis=1),
                ],
                axis=0,
            )
        for k in range(ROW):
            to = lax.rem(x + k, ROW)
            b = i * ROW + to

            @pl.when(b != me)
            def _():
                remote(out_send.at[b], mine_ref.at[me], o_ssem, o_rsem, at(to, zb * SIDE + i)).start()

    with jax.named_scope("class_rows"):
        each(0, SIDE, class_row)
    mine_ref[me] = out_send[me]
    out_size = (NP - 1) * out_send.shape[1]
    with jax.named_scope("take_out"):
        drain(o_rsem, out_size)
    swap = remote(mine_ref, other_ref, c_ssem, c_rsem, partner)
    swap.start()

    drain(g_ssem, (SIDE - 1) * (bundle_size + ROW * kb // 2) + SIDE * (ROW - 1) * (bundle_size + kb // 2))
    drain(lse_ssem, NP - 1)
    drain(o_ssem, out_size)

    @pl.when(owner < OWNERS)
    def _():
        drain(rs_ssem, (OWNERS - 1) * share_size)
        drain(ag_ssem, (nb - 1) * (ag_send.shape[0] + top_send.shape[0]))

    @pl.when(owner >= OWNERS)
    def _():
        drain(rs_ssem, OWNERS * share_size)

    with jax.named_scope("swap"):
        swap.wait()


def finish(mine_ref, other_ref, ev_ref, cs_ref, cw_ref, out_ref):
    coef, kb = cw_ref.shape[0], cs_ref.shape[0] // NP
    halves = []
    for b in range(NP):
        both = mine_ref[b] + other_ref[b]
        cs_ref[b * kb : (b + 1) * kb, :] = both[:kb]
        halves.append(both[kb:])
    for first in range(0, NP, NP // 2):
        turned = jnp.concatenate(halves[first : first + NP // 2], axis=0).T
        for k in range(NP // 2):
            lanes = slice(k * kb // 2, (k + 1) * kb // 2)
            to = (first + k) * kb
            cw_ref[:, to : to + kb // 2] = turned[:coef, lanes]
            cw_ref[:, to + kb // 2 : to + kb] = turned[coef:, lanes]
    out_ref[...] = ev_ref[:, : out_ref.shape[1]]


def body(nz, particles, classes, ctf, sigma2, shell_of, rot_table, ctf_group):
    count, coef = particles.shape[0], shell_of.shape[0]
    classes_n, rotations = classes.shape[0], rot_table.shape[0]
    nb = nz // SIDE
    kb = classes_n // NP
    half = rotations // 2
    pairs = half * kb
    piece = pairs // OWNERS * 2 // 3
    dma = pltpu.SemaphoreType.DMA
    regular = pltpu.SemaphoreType.REGULAR
    vmem = pltpu.VMEM
    i32 = jnp.int32
    arrays = (
        particles,
        classes,
        ctf,
        sigma2.reshape(1, -1),
        shell_of.reshape(1, -1),
        rot_table,
        ctf_group.reshape(1, -1),
    )
    mine, other, evidence = pl.pallas_call(
        functools.partial(kernel, nz),
        out_shape=[
            jax.ShapeDtypeStruct((NP, 24, LANES), F32),
            jax.ShapeDtypeStruct((NP, 24, LANES), F32),
            jax.ShapeDtypeStruct((1, LANES), F32),
        ],
        in_specs=[pl.BlockSpec(memory_space=pltpu.HBM)] * 7,
        out_specs=[pl.BlockSpec(memory_space=vmem)] * 3,
        scratch_shapes=[
            *[vmem(a.shape, a.dtype) for a in arrays[1:]],
            vmem((NP, count + half + 24, LANES), BF16),
            vmem((SIDE, ROW * kb, LANES), BF16),
            vmem((NP, kb, LANES), BF16),
            vmem((NP * coef, half * LANES), BF16),
            vmem((SIDE, ROW * 5 * LANES, 2 * LANES), BF16),
            vmem((NP, 2 * LANES, 3 * LANES), BF16),
            vmem((NP // 4, 8 * kb, 4 * coef), BF16),
            vmem((SIDE, pairs, ROW * 5 * LANES), BF16),
            vmem((pairs, 2 * LANES), F32),
            vmem((OWNERS, piece, LANES), i32),
            vmem((OWNERS, 4, LANES), F32),
            vmem((nb, piece, LANES), i32),
            vmem((nb, 4, LANES), F32),
            vmem((piece, LANES), i32),
            vmem((2, LANES), F32),
            vmem((OWNERS, piece, LANES), i32),
            vmem((OWNERS, 2, LANES), F32),
            vmem((1, LANES), F32),
            vmem((NP, 1, LANES), F32),
            vmem((pairs, 2 * LANES), BF16),
            vmem((ROW, 3 * kb, half * LANES), BF16),
            vmem((NP, 24, LANES), F32),
            vmem((1152, 1, LANES), F32),
            dma((len(arrays) + 1,)),
            dma,
            dma((SIDE,)),
            dma((NP,)),
            dma,
            dma((nb,)),
            dma,
            dma((OWNERS,)),
            dma((OWNERS,)),
            *[dma] * 6,
            regular((OWNERS,)),
        ],
        compiler_params=pltpu.CompilerParams(
            collective_id=0, has_side_effects=True, vmem_limit_bytes=40 * 1024 * 1024
        ),
        name="averaging",
    )(*[pltpu.with_memory_space_constraint(a, pltpu.HBM) for a in arrays])
    sums, weights, evidence = pl.pallas_call(
        finish,
        out_shape=[
            jax.ShapeDtypeStruct((classes_n, 2 * coef), F32),
            jax.ShapeDtypeStruct((coef, classes_n), F32),
            jax.ShapeDtypeStruct((1, count), F32),
        ],
        in_specs=[pl.BlockSpec(memory_space=vmem)] * 3,
        out_specs=[pl.BlockSpec(memory_space=vmem)] * 3,
        compiler_params=pltpu.CompilerParams(vmem_limit_bytes=4 * 1024 * 1024),
        name="finish",
    )(mine, other, evidence)
    return sums, weights.T, evidence.reshape(-1)


def solution(mesh):
    nz = mesh.shape["shell"] // ROW
    split = Mesh(mesh.devices.reshape(mesh.shape["groups"], ROW, nz, mesh.shape["batch"]), AXES)
    shell = ("x", "z")
    placed = (
        P(("groups", "batch"), shell),
        P("groups", shell),
        P("groups", shell),
        P("groups"),
        P(shell),
        P(None, shell),
        P(("groups", "batch")),
    )
    return jax.shard_map(
        functools.partial(body, nz),
        mesh=split,
        in_specs=placed,
        out_specs=(P("groups", shell), P("groups", shell), P(("groups", "batch"))),
        check_vma=False,
    )
```

time: 628 us -> 106 us (0.17)
  waiting for transfers between devices: 372 us -> 0 us
  blocking collectives: 158 us -> 0 us
  Pallas kernels: 0 us -> 106 us
  local copies, waits for them, and re-layouts: 54.5 us -> 0 us
  matrix products: 18.5 us -> 0 us
  between operations: 14.1 us -> 0.64 us
  other arithmetic: 6.99 us -> 0 us
    all_gather x1 -> x0, waiting for transfers between devices: 173 us -> none  [all_blocks(): tiles = lax.all_gather(tiles, axes[k])]
    all_gather x2 -> x0, blocking collectives: 134 us -> none  [the longest x1 124 us: collected_together(): both, at, found = (lax.all_gather(jnp.concatenate(lines), axis), 0, {})]
    unnamed x4 -> x0, waiting for transfers between devices: 114 us -> none
    pallas_call x0 -> x2, Pallas kernels: none -> 106 us  [the longest x1 105 us: body(): pl.pallas_call(functools.partial(kernel, nz), out_shape=[jax.ShapeDtypeSt...]
    reduce_scatter x1 -> x0, waiting for transfers between devices: 86.2 us -> none  [scatter_axes(): nearer = lax.psum_scatter(shard, axes[0], scatter_dimension=dim, tiled=True)]
    all_to_all x1 -> x0, blocking collectives: 24.8 us -> none  [sent_to_all(): lax.all_to_all(jnp.broadcast_to(shard[None], (count, *shard.shape)), axis...]
    dot_general x7 -> x0, matrix products: 18.5 us -> none  [the longest x1 5.89 us: body(): lax.dot_general(ctf_power, class_power, (((1,), (1,)), ((), ())), precisi...]
    reshape x3 -> x0, local copies, waits for them, and re-layouts: 14.6 us -> none  [the longest x1 9.77 us: body(): jnp.transpose(rotated, (0, 2, 1, 3))]
  transfers between devices with their start and end apart: 3 -> 0, of which waited for: 3 -> 0; matrix products, arithmetic and copies ran while one was open for 0% -> 0% of each run, Pallas kernels for 0% -> 0%
where the time goes in v1:
time: 106 us
  Pallas kernels  106 us (100%)
    pallas_call x1, Pallas kernels, body(): pl.pallas_call(functools.partial(kernel, nz), out_shape=[jax.ShapeDtypeSt...  105 us

profile of v1, /device:TPU:33, one launch (start us, length us, event | category | flops | bytes accessed | tf_op | source)
XLA Modules:
  0.0 106.3 jit_solution(14362126452483914312)
XLA Ops:
  0.6 104.6 %averaging.1 = (f32[16,24,128]{2,1,0:T(8,128)S(1)}, f32[16,24,128]{2,1,0:T(8,128)S(1)}, f32[1,128]{1,0:T(1,128)S(1)}) custom-call(bf16[80,128]{1,0:T(8,128)(2,1)} %part_hbm.1, bf16[256,128]{1,0:T(8,128)(2,1)} %cls_hbm.1, f32[8,64]{1,0:T(8,128)} %ctf_hbm.1, f32[1,64]{1,0:T(1,128)} %bitcast.5, s32[1,64]{1,0:T(1,128)} %bitcast.6, s32[48,64]{1,0:T(8,128)} %tab_hbm.1, ...), custom_call_target="tpu_custom_call" | custom-call | tf_op jit(solution)/shard_map/averaging/pallas_call | solution.py:573
  105.2 1.1 %finish.1 = (f32[256,128]{1,0:T(8,128)}, f32[64,256]{1,0:T(8,128)}, f32[1,80]{1,0:T(1,128)}) custom-call(f32[16,24,128]{2,1,0:T(8,128)S(1)} %get-tuple-element.9.mine_ref, f32[16,24,128]{2,1,0:T(8,128)S(1)} %get-tuple-element.10.other_ref, f32[1,128]{1,0:T(1,128)S(1)} %get-tuple-element.11.ev_ref), custom_call_target="tpu_custom_call" | custom-call | tf_op jit(solution)/shard_map/finish/pallas_call | solution.py:624

commit v2 on v1

--- a/solution.py
+++ b/solution.py
@@ -127,7 +127,11 @@
     o_rsem,
     c_ssem,
     c_rsem,
+    column_in,
+    others_in,
     owner_in,
+    first_in,
+    partner_in,
 ):
     nb = nz // SIDE
     count, coef = part_hbm.shape[0], ctf_ref.shape[1]
@@ -140,17 +144,24 @@
     core = lax.axis_index("batch")
     zb, zi = z // SIDE, lax.rem(z, SIDE)
     me = zi * ROW + x
-    owner = jnp.where(
-        jnp.logical_and(zb >= 1, zb < 3), zb - 1, jnp.where(jnp.logical_and(zb >= nb - 3, zb < nb - 1), zb - nb + 5, OWNERS)
-    )
+    def owns(b):
+        return jnp.logical_or(
+            jnp.logical_and(b >= 1, b < 3), jnp.logical_and(b >= nb - 3, b < nb - 1)
+        )
 
     def home(o):
         return jnp.where(o < 2, o + 1, o + nb - 5)
 
-    def turn_in(b):
-        return jnp.where(b == 0, nb - 2, jnp.where(b == nb - 1, nb - 1, b - 1))
-
-    my_turn = turn_in(zb)
+    owner = jnp.where(owns(zb), jnp.where(zb < 3, zb - 1, zb - nb + 5), OWNERS)
+
+    def greets(a, b):
+        between = jnp.logical_and(jnp.logical_and(a >= 1, a < b), b < nb - 1)
+        return jnp.logical_or(
+            jnp.logical_and(between, jnp.logical_or(owns(a), owns(b))),
+            jnp.logical_or(
+                jnp.logical_and(b == 0, jnp.logical_and(a >= 1, a < 3)), jnp.logical_and(b == nb - 1, owns(a))
+            ),
+        )
 
     def at(x_, z_):
         return (group, x_, z_, core)
@@ -193,15 +204,19 @@
         load.start()
 
     barrier = pltpu.get_barrier_semaphore()
-    each(1, NP, lambda k: tell(barrier, mate(k)[1]))
-    tell(barrier, partner)
-
-    def greet_later(b):
-        @pl.when(turn_in(b) > my_turn)
+    each(1, ROW, lambda k: tell(barrier, at(lax.rem(x + k, ROW), z)))
+    each((zi + 1) * ROW, NP, lambda i: tell(barrier, at(lax.rem(i, ROW), zb * SIDE + i // ROW)))
+
+    @pl.when(core > 0)
+    def _():
+        tell(barrier, partner)
+
+    def greet(b):
+        @pl.when(greets(zb, b))
         def _():
             tell(barrier, far(b))
 
-    each(0, nb, greet_later)
+    each(0, nb, greet)
     for load in loads[:4]:
         load.wait()
 
@@ -221,10 +236,10 @@
     for load in loads[4:]:
         load.wait()
     with jax.named_scope("barrier"):
-        pl.semaphore_wait(barrier, NP + my_turn)
-
-    def down(k):
-        i = lax.rem(zi + k, SIDE)
+        greeted = sum(jnp.where(greets(b, zb), 1, 0) for b in range(nb))
+        pl.semaphore_wait(barrier, ROW - 1 + zi * ROW + jnp.where(core > 0, 0, 1) + greeted)
+
+    def down(i):
         device = at(x, zb * SIDE + i)
         remote(bundle.at[me], bundle.at[me], g_ssem, z_rsem.at[zi], device).start()
         remote(cls_ref.at[rows_of(i, ROW * kb)], cls_z.at[zi], g_ssem, z_rsem.at[zi], device).start()
@@ -238,17 +253,30 @@
             remote(cls_z.at[i, rows_of(to, kb)], cls_all.at[b], g_ssem, x_rsem.at[b], device).start()
 
     bundle_size = bundle.shape[1] // 2
-    each(1, SIDE, down)
+    def tell_above(i):
+        tell(column_in.at[zi], at(x, zb * SIDE + i))
+        each(1, ROW, lambda k: tell(others_in, at(lax.rem(x + k, ROW), zb * SIDE + i)))
+
+    each(0, zi, tell_above)
+    each(0, zi, lambda k: down(zi - 1 - k))
     across(zi)
 
     @pl.when(owner < OWNERS)
     def _():
         def tell_earlier(b):
-            @pl.when(turn_in(b) < my_turn)
+            @pl.when(greets(b, zb))
             def _():
                 tell(owner_in.at[owner], far(b))
 
         each(0, nb, tell_earlier)
+
+    @pl.when(zb == 0)
+    def _():
+        tell(first_in, far(1))
+
+    @pl.when(core == 0)
+    def _():
+        tell(partner_in, partner)
 
     with jax.named_scope("zeros"):
         w_all[...] = jnp.zeros_like(w_all)
@@ -261,12 +289,10 @@
     low_kb = lane((kb, LANES)) < coef
 
     def pass_on(i):
-        @pl.when(i != zi)
-        def _():
-            with jax.named_scope("came_down"):
-                drain(z_rsem.at[i], bundle_size + ROW * kb // 2)
-            across(i)
-            cls_all[i * ROW + x] = cls_z[i, rows_of(x, kb), :]
+        with jax.named_scope("came_down"):
+            drain(z_rsem.at[i], bundle_size + ROW * kb // 2)
+        across(i)
+        cls_all[i * ROW + x] = cls_z[i, rows_of(x, kb), :]
 
     def amplitudes(tail):
         par = tail[half : half + 8] + tail[half + 8 : half + 16] + tail[half + 16 : half + 24]
@@ -280,18 +306,17 @@
         return jnp.concatenate([a, jnp.zeros((LANES - count, LANES), F32)], axis=0).astype(BF16).T
 
     def prepare(g, i):
-        b = g * 4 + i
+        b = g * ROW + i
         landing = bundle[b, count:].astype(F32)
         amp, wamp = amplitudes(landing)
         weighted = turned_over(wamp * bundle[b, 0:count].astype(F32))
         pen = -0.5 * (wamp * amp)
         pen_hi = pen.astype(BF16).astype(F32)
         pen = turned_over(jnp.where(low, pen_hi, pen - pen_hi))
-        for s in range(2):
-            lanes = slice(s * LANES, (s + 1) * LANES)
-            for k, piece in enumerate((weighted[:coef], weighted[coef:], pen[:coef], pen[:coef], pen[coef:])):
-                top = (5 * i + k) * LANES + s * coef
-                w_all[g, top : top + coef, lanes] = piece
+        for k, piece in enumerate((weighted[:coef], weighted[coef:], pen[:coef], pen[:coef], pen[coef:])):
+            for s in range(2):
+                top = pl.multiple_of((5 * b + k) * LANES + s * coef, coef)
+                w_all[pl.ds(top, coef), s * LANES : (s + 1) * LANES] = piece
         index = lax.broadcasted_iota(jnp.int32, (coef, LANES), 0).astype(F32).astype(BF16)
         ones, zeros = jnp.ones((coef, LANES), BF16), jnp.zeros((coef, LANES), BF16)
         for j in range(half):
@@ -328,7 +353,7 @@
         lhs = left[g]
         for jj in range(half // 2):
             turned = jnp.dot(
-                lhs, place[rows_of(g, 4 * coef), jj * 256 : (jj + 1) * 256], preferred_element_type=F32
+                lhs, place[g * 4 * coef : (g + 1) * 4 * coef, jj * 256 : (jj + 1) * 256], preferred_element_type=F32
             )
             for i in range(4):
                 for t in range(2):
@@ -341,29 +366,48 @@
                     to = slice(j * kb, (j + 1) * kb)
                     pieces = re.astype(BF16), im.astype(BF16), power_hi, power_lo, power_hi
                     for k, piece in enumerate(pieces):
-                        at_lane = (5 * i + k) * LANES
-                        rot_all[g, to, at_lane : at_lane + LANES] = piece
-
-    def score_row(g):
+                        at_lane = (5 * (g * ROW + i) + k) * LANES
+                        rot_all[to, at_lane : at_lane + LANES] = piece
+
+    def score_rows(rows_in):
         with jax.named_scope("arrive"):
-            each(1, ROW, lambda k: drain(x_rsem.at[g * ROW + lax.rem(x + k, ROW)], bundle_size + kb // 2))
-        with jax.named_scope("prepare"):
-            for i in range(ROW):
-                prepare(g, i)
+            for g in rows_in:
+                each(1, ROW, lambda k: drain(x_rsem.at[g * ROW + lax.rem(x + k, ROW)], bundle_size + kb // 2))
         with jax.named_scope("scores"):
-            rotate(g)
-            score[...] += jnp.dot(rot_all[g], w_all[g], preferred_element_type=F32)
-
-    each(0, SIDE - 1, pass_on)
-
-    def turn_of(g):
-        @pl.when(g == 1)
+            for g in rows_in:
+                for k in range(1, ROW):
+                    prepare(g, lax.rem(x + k, ROW))
+            for g in rows_in:
+                rotate(g)
+            depth = slice(rows_in[0] * ROW * 5 * LANES, (rows_in[-1] + 1) * ROW * 5 * LANES)
+            score[...] += jnp.dot(rot_all[:, depth], w_all[depth, :], preferred_element_type=F32)
+
+    prepare(zi, x)
+
+    def down_later(i):
+        pl.semaphore_wait(column_in.at[i], 1)
+        down(i)
+
+    with jax.named_scope("down_later"):
+        each(zi + 1, SIDE, down_later)
+    nearest = (1, 0, 1, 2), (2, 2, 0, 1), (3, 3, 3, 0)
+    for step in nearest:
+        i = sum(jnp.where(zi == k, step[k], 0) for k in range(SIDE))
+        pass_on(i)
+        prepare(i, x)
+
+    def half_of_rows(step):
+        first = (zi == SIDE - 1) == (step == 0)
+
+        @pl.when(first)
         def _():
-            pass_on(SIDE - 1)
-
-        score_row(g)
-
-    each(0, SIDE, turn_of)
+            score_rows([SIDE - 1])
+
+        @pl.when(jnp.logical_not(first))
+        def _():
+            score_rows(list(range(SIDE - 1)))
+
+    each(0, 2, half_of_rows)
 
     def share(o):
         return score[rows_of(o, rows), :]
@@ -385,7 +429,7 @@
             rs_send[o] = compact((one & 0xFFFF) | (two << 16))
             rs_scale[o] = jnp.concatenate([*spread(reach * (1.0 / 32767.0)), *spread(middle)], axis=0)
 
-            @pl.when(turn_in(home(o)) > my_turn)
+            @pl.when(jnp.logical_not(greets(home(o), zb)))
             def _():
                 with jax.named_scope("owner_in"):
                     pl.semaphore_wait(owner_in.at[o], 1)
@@ -394,8 +438,21 @@
                 remote(rs_send.at[o], rs_recv.at[zb], rs_ssem, rs_rsem.at[zb], far(home(o))).start()
                 remote(rs_scale.at[o], rs_rscale.at[zb], rs_ssem, rs_rsem.at[zb], far(home(o))).start()
 
+    @pl.when(zb == 1)
+    def _():
+        pl.semaphore_wait(first_in, 1)
+        tell(owner_in.at[2], far(0))
+        tell(owner_in.at[3], far(0))
+
     with jax.named_scope("sources"):
         each(0, NP, prepare_sources)
+
+    urgent = jnp.where(zb < nb // 2, nb, nb - 2)
+
+    def send_post(b):
+        @pl.when(b != zb)
+        def _():
+            remote(ag_send, ag_recv.at[owner], ag_ssem, ag_rsem.at[owner], far(b)).start()
 
     @pl.when(owner < OWNERS)
     def _():
@@ -431,12 +488,7 @@
         two = (exp_two * 65535.0 + 0.5).astype(jnp.int32)
         ag_send[...] = (one & 0xFFFF) | (two << 16)
 
-        def send_post(b):
-            @pl.when(b != zb)
-            def _():
-                remote(ag_send, ag_recv.at[owner], ag_ssem, ag_rsem.at[owner], far(b)).start()
-
-        each(0, nb, send_post)
+        each(0, urgent, send_post)
         ag_recv[owner] = ag_send[...]
         top_recv[owner] = top_send[...]
 
@@ -454,8 +506,18 @@
 
     evidence = merged([top_recv[o, 1:2] for o in range(OWNERS)])
     lse_own[...] = evidence
+
+    @pl.when(zi < SIDE - 1)
+    def _():
+        pl.semaphore_wait(others_in, (SIDE - 1 - zi) * (ROW - 1))
+
     each(1, NP, lambda k: remote(lse_own, lse_all.at[me], lse_ssem, lse_rsem, mate(k)[1]).start())
     lse_all[me] = evidence
+
+    @pl.when(owner < OWNERS)
+    def _():
+        each(urgent, nb, send_post)
+
     with jax.named_scope("lse_in"):
         drain(lse_rsem, NP - 1)
     everyone = lse_all[...]
@@ -512,6 +574,11 @@
     out_size = (NP - 1) * out_send.shape[1]
     with jax.named_scope("take_out"):
         drain(o_rsem, out_size)
+
+    @pl.when(core > 0)
+    def _():
+        pl.semaphore_wait(partner_in, 1)
+
     swap = remote(mine_ref, other_ref, c_ssem, c_rsem, partner)
     swap.start()
 
@@ -585,10 +652,10 @@
             vmem((SIDE, ROW * kb, LANES), BF16),
             vmem((NP, kb, LANES), BF16),
             vmem((NP * coef, half * LANES), BF16),
-            vmem((SIDE, ROW * 5 * LANES, 2 * LANES), BF16),
+            vmem((NP * 5 * LANES, 2 * LANES), BF16),
             vmem((NP, 2 * LANES, 3 * LANES), BF16),
             vmem((NP // 4, 8 * kb, 4 * coef), BF16),
-            vmem((SIDE, pairs, ROW * 5 * LANES), BF16),
+            vmem((pairs, NP * 5 * LANES), BF16),
             vmem((pairs, 2 * LANES), F32),
             vmem((OWNERS, piece, LANES), i32),
             vmem((OWNERS, 4, LANES), F32),
@@ -614,7 +681,11 @@
             dma((OWNERS,)),
             dma((OWNERS,)),
             *[dma] * 6,
+            regular((SIDE,)),
+            regular,
             regular((OWNERS,)),
+            regular,
+            regular,
         ],
         compiler_params=pltpu.CompilerParams(
             collective_id=0, has_side_effects=True, vmem_limit_bytes=40 * 1024 * 1024

time: 106 us -> 105 us (level)
  Pallas kernels: 106 us -> 104 us
    pallas_call x1, Pallas kernels: 105 us -> 103 us  [body(): pl.pallas_call(functools.partial(kernel, nz), out_shape=[jax.ShapeDtypeSt...]
where the time goes in v2:
time: 105 us
  Pallas kernels  104 us (99%)
    pallas_call x1, Pallas kernels, body(): pl.pallas_call(functools.partial(kernel, nz), out_shape=[jax.ShapeDtypeSt...  103 us

profile of v2, /device:TPU:33, one launch (start us, length us, event | category | flops | bytes accessed | tf_op | source)
XLA Modules:
  0.0 104.5 jit_solution(4296804199223842121)
XLA Ops:
  0.6 102.8 %averaging.1 = (f32[16,24,128]{2,1,0:T(8,128)S(1)}, f32[16,24,128]{2,1,0:T(8,128)S(1)}, f32[1,128]{1,0:T(1,128)S(1)}) custom-call(bf16[80,128]{1,0:T(8,128)(2,1)} %part_hbm.1, bf16[256,128]{1,0:T(8,128)(2,1)} %cls_hbm.1, f32[8,64]{1,0:T(8,128)} %ctf_hbm.1, f32[1,64]{1,0:T(1,128)} %bitcast.5, s32[1,64]{1,0:T(1,128)} %bitcast.6, s32[48,64]{1,0:T(8,128)} %tab_hbm.1, ...), custom_call_target="tpu_custom_call" | custom-call | tf_op jit(solution)/shard_map/averaging/pallas_call | solution.py:640
  103.5 1.1 %finish.1 = (f32[256,128]{1,0:T(8,128)}, f32[64,256]{1,0:T(8,128)}, f32[1,80]{1,0:T(1,128)}) custom-call(f32[16,24,128]{2,1,0:T(8,128)S(1)} %get-tuple-element.9.mine_ref, f32[16,24,128]{2,1,0:T(8,128)S(1)} %get-tuple-element.10.other_ref, f32[1,128]{1,0:T(1,128)S(1)} %get-tuple-element.11.ev_ref), custom_call_target="tpu_custom_call" | custom-call | tf_op jit(solution)/shard_map/finish/pallas_call | solution.py:695

commit v3 on v2

--- a/solution.py
+++ b/solution.py
@@ -93,6 +93,7 @@
     cls_z,
     cls_all,
     place,
+    place_turned,
     w_all,
     src_all,
     left,
@@ -106,6 +107,8 @@
     top_send,
     ag_recv,
     top_recv,
+    lse_send,
+    lse_first,
     lse_own,
     lse_all,
     post,
@@ -119,8 +122,10 @@
     rs_ssem,
     rs_rsem,
     ag_ssem,
+    pass_ssem,
     ag_rsem,
     top_rsem,
+    first_rsem,
     lse_ssem,
     lse_rsem,
     o_ssem,
@@ -221,12 +226,11 @@
         load.wait()
 
     levels = sig_ref.shape[1]
-    pick = (lax.broadcasted_iota(jnp.int32, (levels, coef), 0) == sh_ref[...]).astype(F32)
-    noise = jnp.dot(
-        jnp.broadcast_to(sig_ref[...], (8, levels)), pick, precision=lax.Precision.HIGHEST, preferred_element_type=F32
-    )
+    pick = lax.broadcasted_iota(jnp.int32, (levels, coef), 0) == sh_ref[...]
+    noise_of = jnp.broadcast_to(sig_ref[...], (coef, levels)).T
+    noise = jnp.sum(jnp.where(pick, noise_of, 0.0), axis=0, keepdims=True)
     ctf = ctf_ref[...]
-    par = jnp.concatenate([ctf, (1.0 / noise[0:1]) * ctf], axis=1)
+    par = jnp.concatenate([ctf, (1.0 / noise) * ctf], axis=1)
     par_high = par.astype(BF16).astype(F32)
     par_mid = (par - par_high).astype(BF16).astype(F32)
     offset = (x * nz + z) * coef
@@ -249,8 +253,8 @@
         for k in range(1, ROW):
             to = lax.rem(x + k, ROW)
             device = at(to, z)
-            remote(bundle.at[b], bundle.at[b], g_ssem, x_rsem.at[b], device).start()
-            remote(cls_z.at[i, rows_of(to, kb)], cls_all.at[b], g_ssem, x_rsem.at[b], device).start()
+            remote(bundle.at[b], bundle.at[b], g_ssem, x_rsem.at[i], device).start()
+            remote(cls_z.at[i, rows_of(to, kb)], cls_all.at[b], g_ssem, x_rsem.at[i], device).start()
 
     bundle_size = bundle.shape[1] // 2
     def tell_above(i):
@@ -315,8 +319,8 @@
         pen = turned_over(jnp.where(low, pen_hi, pen - pen_hi))
         for k, piece in enumerate((weighted[:coef], weighted[coef:], pen[:coef], pen[:coef], pen[coef:])):
             for s in range(2):
-                top = pl.multiple_of((5 * b + k) * LANES + s * coef, coef)
-                w_all[pl.ds(top, coef), s * LANES : (s + 1) * LANES] = piece
+                top = pl.multiple_of((5 * i + k) * LANES + s * coef, coef)
+                w_all[g, pl.ds(top, coef), s * LANES : (s + 1) * LANES] = piece
         index = lax.broadcasted_iota(jnp.int32, (coef, LANES), 0).astype(F32).astype(BF16)
         ones, zeros = jnp.ones((coef, LANES), BF16), jnp.zeros((coef, LANES), BF16)
         for j in range(half):
@@ -324,20 +328,28 @@
             row = jnp.concatenate([row] * (coef // 16), axis=0)
             place[rows_of(b, coef), j * LANES : (j + 1) * LANES] = jnp.where(index == row, ones, zeros)
 
-    def prepare_sources(b):
-        amp, _ = amplitudes(bundle[b, count:].astype(F32))
-        source = amp * bundle[b, 0:count].astype(F32)
-        source_turned = pltpu.roll(source, coef, 1)
-        power = amp * amp
-        for s in range(2):
-            top = s * LANES
-
-            def keep(lower, upper):
-                return (jnp.where(low, lower, 0.0) if s == 0 else jnp.where(low, 0.0, upper)).astype(BF16)
-
-            src_all[b, top : top + count, 0:128] = keep(source, source_turned)
-            src_all[b, top : top + count, 128:256] = keep(source_turned, source)
-            src_all[b, top : top + count, 256:384] = keep(power, power)
+    def prepare_sources(pair):
+        for i in range(2):
+            b = pair * 2 + i
+            amp, _ = amplitudes(bundle[b, count:].astype(F32))
+            source = amp * bundle[b, 0:count].astype(F32)
+            source_turned = pltpu.roll(source, coef, 1)
+            power = amp * amp
+            for s in range(2):
+                top = s * LANES
+
+                def keep(lower, upper):
+                    return (jnp.where(low, lower, 0.0) if s == 0 else jnp.where(low, 0.0, upper)).astype(BF16)
+
+                for t, kept in (
+                    (2 * i, keep(source, source_turned)),
+                    (2 * i + 1, keep(source_turned, source)),
+                    (4 + i, keep(power, power)),
+                ):
+                    src_all[pair, top : top + count, t * LANES : (t + 1) * LANES] = kept
+        for j in range(half):
+            lanes = slice(j * LANES, (j + 1) * LANES)
+            place_turned[pair, lanes, :] = place[rows_of(pair, 2 * coef), lanes].T
 
     def rotate(g):
         for i in range(4):
@@ -353,7 +365,7 @@
         lhs = left[g]
         for jj in range(half // 2):
             turned = jnp.dot(
-                lhs, place[g * 4 * coef : (g + 1) * 4 * coef, jj * 256 : (jj + 1) * 256], preferred_element_type=F32
+                lhs, place[rows_of(g, 4 * coef), jj * 256 : (jj + 1) * 256], preferred_element_type=F32
             )
             for i in range(4):
                 for t in range(2):
@@ -366,21 +378,17 @@
                     to = slice(j * kb, (j + 1) * kb)
                     pieces = re.astype(BF16), im.astype(BF16), power_hi, power_lo, power_hi
                     for k, piece in enumerate(pieces):
-                        at_lane = (5 * (g * ROW + i) + k) * LANES
-                        rot_all[to, at_lane : at_lane + LANES] = piece
-
-    def score_rows(rows_in):
+                        at_lane = (5 * i + k) * LANES
+                        rot_all[g, to, at_lane : at_lane + LANES] = piece
+
+    def score_row(g):
         with jax.named_scope("arrive"):
-            for g in rows_in:
-                each(1, ROW, lambda k: drain(x_rsem.at[g * ROW + lax.rem(x + k, ROW)], bundle_size + kb // 2))
+            drain(x_rsem.at[g], (ROW - 1) * (bundle_size + kb // 2))
         with jax.named_scope("scores"):
-            for g in rows_in:
-                for k in range(1, ROW):
-                    prepare(g, lax.rem(x + k, ROW))
-            for g in rows_in:
-                rotate(g)
-            depth = slice(rows_in[0] * ROW * 5 * LANES, (rows_in[-1] + 1) * ROW * 5 * LANES)
-            score[...] += jnp.dot(rot_all[:, depth], w_all[depth, :], preferred_element_type=F32)
+            for k in range(1, ROW):
+                prepare(g, lax.rem(x + k, ROW))
+            rotate(g)
+            score[...] += jnp.dot(rot_all[g], w_all[g], preferred_element_type=F32)
 
     prepare(zi, x)
 
@@ -390,24 +398,28 @@
 
     with jax.named_scope("down_later"):
         each(zi + 1, SIDE, down_later)
-    nearest = (1, 0, 1, 2), (2, 2, 0, 1), (3, 3, 3, 0)
-    for step in nearest:
-        i = sum(jnp.where(zi == k, step[k], 0) for k in range(SIDE))
-        pass_on(i)
-        prepare(i, x)
-
-    def half_of_rows(step):
-        first = (zi == SIDE - 1) == (step == 0)
-
-        @pl.when(first)
-        def _():
-            score_rows([SIDE - 1])
-
-        @pl.when(jnp.logical_not(first))
-        def _():
-            score_rows(list(range(SIDE - 1)))
-
-    each(0, 2, half_of_rows)
+
+    nearest = (0, 1, 2, 3), (1, 0, 1, 2), (2, 2, 0, 1), (3, 3, 3, 0)
+
+    def place_of(step):
+        return sum(
+            jnp.where(jnp.logical_and(step == t, zi == k), nearest[t][k], 0) for t in range(SIDE) for k in range(SIDE)
+        )
+
+    def turn_of(step):
+        @pl.when(step == 1)
+        def _():
+            for t in range(1, SIDE):
+                pass_on(place_of(t))
+                prepare(place_of(t), x)
+
+        score_row(place_of(step))
+
+    each(0, SIDE, turn_of)
+
+    @pl.when(zi < SIDE - 1)
+    def _():
+        pl.semaphore_wait(others_in, (SIDE - 1 - zi) * (ROW - 1))
 
     def share(o):
         return score[rows_of(o, rows), :]
@@ -445,9 +457,9 @@
         tell(owner_in.at[3], far(0))
 
     with jax.named_scope("sources"):
-        each(0, NP, prepare_sources)
-
-    urgent = jnp.where(zb < nb // 2, nb, nb - 2)
+        each(0, NP // 2, prepare_sources)
+
+    later = zb >= nb // 2
 
     def send_post(b):
         @pl.when(b != zb)
@@ -477,57 +489,91 @@
         exp_one, exp_two = jnp.exp(total_one - shift), jnp.exp(total_two - shift)
         evidence = peak + jnp.log(over_rows(exp_one + exp_two, jnp.add, jnp.sum))
         top_send[...] = jnp.concatenate([peak, evidence], axis=0)
+        lse_send[...] = evidence
+
+        each(
+            0,
+            NP,
+            lambda k: remote(
+                lse_send, lse_first.at[owner * NP + me], ag_ssem, first_rsem, at(lax.rem(k, ROW), k // ROW)
+            ).start(),
+        )
 
         def send_top(b):
             @pl.when(b != zb)
             def _():
-                remote(top_send, top_recv.at[owner], ag_ssem, top_rsem.at[owner], far(b)).start()
+                remote(top_send, top_recv.at[owner], ag_ssem, top_rsem, far(b)).start()
 
         each(0, nb, send_top)
         one = (exp_one * 65535.0 + 0.5).astype(jnp.int32)
         two = (exp_two * 65535.0 + 0.5).astype(jnp.int32)
         ag_send[...] = (one & 0xFFFF) | (two << 16)
 
-        each(0, urgent, send_post)
+
+        def send_early(b):
+            @pl.when(jnp.logical_not(jnp.logical_and(later, b == 1)))
+            def _():
+                send_post(b)
+
+        each(0, nb - 2, send_early)
         ag_recv[owner] = ag_send[...]
         top_recv[owner] = top_send[...]
 
-    def take_top(o):
-        @pl.when(o != owner)
-        def _():
-            with jax.named_scope("top_in"):
-                drain(top_rsem.at[o], top_send.shape[0])
-
-    each(0, OWNERS, take_top)
-
-    def merged(parts):
-        most = functools.reduce(jnp.maximum, parts)
-        return most + jnp.log(functools.reduce(jnp.add, [jnp.exp(e - most) for e in parts]))
-
-    evidence = merged([top_recv[o, 1:2] for o in range(OWNERS)])
-    lse_own[...] = evidence
-
-    @pl.when(zi < SIDE - 1)
-    def _():
-        pl.semaphore_wait(others_in, (SIDE - 1 - zi) * (ROW - 1))
-
-    each(1, NP, lambda k: remote(lse_own, lse_all.at[me], lse_ssem, lse_rsem, mate(k)[1]).start())
-    lse_all[me] = evidence
-
-    @pl.when(owner < OWNERS)
-    def _():
-        each(urgent, nb, send_post)
-
-    with jax.named_scope("lse_in"):
-        drain(lse_rsem, NP - 1)
-    everyone = lse_all[...]
-    most = jnp.max(everyone, axis=0)
-    evidence = most + jnp.log(jnp.sum(jnp.exp(everyone - most[None]), axis=0))
-    ev_ref[...] = evidence
+    with jax.named_scope("top_in"):
+
+        @pl.when(owner < OWNERS)
+        def _():
+            drain(top_rsem, (OWNERS - 1) * top_send.shape[0])
+
+        @pl.when(owner >= OWNERS)
+        def _():
+            drain(top_rsem, OWNERS * top_send.shape[0])
+
+    def merged(parts, axis):
+        most = jnp.max(parts, axis=axis, keepdims=True)
+        return most + jnp.log(jnp.sum(jnp.exp(parts - most), axis=axis, keepdims=True))
+
+    @pl.when(jnp.logical_and(owner < OWNERS, later))
+    def _():
+        each(nb - 2, nb, send_post)
+
+    def pass_post(o, b):
+        with jax.named_scope("post_in"):
+            drain(ag_rsem.at[o], ag_send.shape[0])
+        remote(ag_recv.at[o], ag_recv.at[o], pass_ssem, ag_rsem.at[o], far(b)).start()
+
+    @pl.when(zb == 0)
+    def _():
+        for o in range(OWNERS):
+            pass_post(o, nb - 1 if o < OWNERS // 2 else 1)
+
+    @pl.when(zb == 0)
+    def _():
+        with jax.named_scope("first_in"):
+            drain(first_rsem, OWNERS * NP)
+        ev_ref[...] = merged(lse_first[...], 0)[0]
+
+    @pl.when(zb > 0)
+    def _():
+        lse_own[...] = merged(jnp.concatenate([top_recv[o, 1:2] for o in range(OWNERS)], axis=0), 0)
+        each(1, NP, lambda k: remote(lse_own, lse_all.at[me], lse_ssem, lse_rsem, mate(k)[1]).start())
+        lse_all[me] = lse_own[...]
+        with jax.named_scope("lse_in"):
+            drain(lse_rsem, NP - 1)
+        drain(lse_ssem, NP - 1)
+        ev_ref[...] = merged(lse_all[...], 0)[0]
+
+    evidence = ev_ref[...]
     used = lane((rows, LANES)) < count
 
     def take_post(o):
-        @pl.when(o != owner)
+        passes = jnp.logical_and(zb == nb - 1, o < OWNERS // 2)
+
+        @pl.when(passes)
+        def _():
+            pass_post(o, nb - 2)
+
+        @pl.when(jnp.logical_not(jnp.logical_or(passes, jnp.logical_or(o == owner, zb == 0))))
         def _():
             with jax.named_scope("post_in"):
                 drain(ag_rsem.at[o], ag_send.shape[0])
@@ -542,24 +588,34 @@
     each(0, OWNERS, take_post)
 
     def class_row(i):
-        for k in range(ROW):
-            frames = jnp.dot(post[...], src_all[i * ROW + k], preferred_element_type=F32)
+        pairs_in = [i * (ROW // 2) + k for k in range(ROW // 2)]
+        for k, pair in enumerate(pairs_in):
+            frames = jnp.dot(post[...], src_all[pair], preferred_element_type=F32)
             for j in range(half):
-                for t in range(3):
-                    frame[k, t * kb : (t + 1) * kb, j * LANES : (j + 1) * LANES] = frames[
+                for t in range(6):
+                    to = ((t // 2) * 3 + t % 2 if t < 4 else (t - 4) * 3 + 2) * kb
+                    frame[k, to : to + kb, j * LANES : (j + 1) * LANES] = frames[
                         j * kb : (j + 1) * kb, t * LANES : (t + 1) * LANES
                     ].astype(BF16)
-        for k in range(ROW):
-            turned = place[rows_of(i * ROW + k, coef), :]
-            sums = lax.dot_general(frame[k], turned, NT, preferred_element_type=F32)
-            weights = sums[2 * kb : 3 * kb]
-            out_send[i * ROW + k] = jnp.concatenate(
-                [
-                    jnp.concatenate([sums[0:kb], sums[kb : 2 * kb]], axis=1),
-                    jnp.concatenate([weights[: kb // 2], weights[kb // 2 :]], axis=1),
-                ],
-                axis=0,
-            )
+        low_out = lane((kb, LANES)) < coef
+        for k, pair in enumerate(pairs_in):
+            sums = jnp.zeros((6 * kb, LANES), F32)
+            for at_depth in range(0, half * LANES, 2 * LANES):
+                depth = slice(at_depth, at_depth + 2 * LANES)
+                sums += jnp.dot(frame[k, :, depth], place_turned[pair, depth, :], preferred_element_type=F32)
+            for t in range(2):
+                mine = sums[3 * t * kb : 3 * (t + 1) * kb]
+                other = pltpu.roll(mine, coef, 1)
+                lower, upper = (mine, other) if t == 0 else (other, mine)
+                out_send[i * ROW + 2 * k + t] = jnp.concatenate(
+                    [
+                        jnp.where(low_out, lower[:kb], upper[kb : 2 * kb]),
+                        jnp.where(
+                            low_out[: kb // 2], lower[2 * kb : 2 * kb + kb // 2], upper[2 * kb + kb // 2 : 3 * kb]
+                        ),
+                    ],
+                    axis=0,
+                )
         for k in range(ROW):
             to = lax.rem(x + k, ROW)
             b = i * ROW + to
@@ -583,13 +639,24 @@
     swap.start()
 
     drain(g_ssem, (SIDE - 1) * (bundle_size + ROW * kb // 2) + SIDE * (ROW - 1) * (bundle_size + kb // 2))
-    drain(lse_ssem, NP - 1)
     drain(o_ssem, out_size)
 
     @pl.when(owner < OWNERS)
     def _():
         drain(rs_ssem, (OWNERS - 1) * share_size)
-        drain(ag_ssem, (nb - 1) * (ag_send.shape[0] + top_send.shape[0]))
+        drain(ag_ssem, (nb - 3) * ag_send.shape[0] + (nb - 1) * top_send.shape[0] + NP)
+
+        @pl.when(later)
+        def _():
+            drain(ag_ssem, ag_send.shape[0])
+
+    @pl.when(zb == 0)
+    def _():
+        drain(pass_ssem, OWNERS * ag_send.shape[0])
+
+    @pl.when(zb == nb - 1)
+    def _():
+        drain(pass_ssem, OWNERS // 2 * ag_send.shape[0])
 
     @pl.when(owner >= OWNERS)
     def _():
@@ -652,10 +719,11 @@
             vmem((SIDE, ROW * kb, LANES), BF16),
             vmem((NP, kb, LANES), BF16),
             vmem((NP * coef, half * LANES), BF16),
-            vmem((NP * 5 * LANES, 2 * LANES), BF16),
-            vmem((NP, 2 * LANES, 3 * LANES), BF16),
+            vmem((NP // 2, half * LANES, 2 * coef), BF16),
+            vmem((SIDE, ROW * 5 * LANES, 2 * LANES), BF16),
+            vmem((NP // 2, 2 * LANES, 6 * LANES), BF16),
             vmem((NP // 4, 8 * kb, 4 * coef), BF16),
-            vmem((pairs, NP * 5 * LANES), BF16),
+            vmem((SIDE, pairs, ROW * 5 * LANES), BF16),
             vmem((pairs, 2 * LANES), F32),
             vmem((OWNERS, piece, LANES), i32),
             vmem((OWNERS, 4, LANES), F32),
@@ -666,21 +734,23 @@
             vmem((OWNERS, piece, LANES), i32),
             vmem((OWNERS, 2, LANES), F32),
             vmem((1, LANES), F32),
+            vmem((OWNERS * NP, 1, LANES), F32),
+            vmem((1, LANES), F32),
             vmem((NP, 1, LANES), F32),
             vmem((pairs, 2 * LANES), BF16),
-            vmem((ROW, 3 * kb, half * LANES), BF16),
+            vmem((ROW // 2, 6 * kb, half * LANES), BF16),
             vmem((NP, 24, LANES), F32),
             vmem((1152, 1, LANES), F32),
             dma((len(arrays) + 1,)),
             dma,
             dma((SIDE,)),
-            dma((NP,)),
+            dma((SIDE,)),
             dma,
             dma((nb,)),
             dma,
+            dma,
             dma((OWNERS,)),
-            dma((OWNERS,)),
-            *[dma] * 6,
+            *[dma] * 8,
             regular((SIDE,)),
             regular,
             regular((OWNERS,)),

time: 105 us -> 99.9 us (0.951)
  Pallas kernels: 104 us -> 99.1 us
    pallas_call x1, Pallas kernels: 103 us -> 98 us  [body(): pl.pallas_call(functools.partial(kernel, nz), out_shape=[jax.ShapeDtypeSt...]
where the time goes in v3:
time: 99.9 us; the launch traced here: 99.7 us
  Pallas kernels  99.1 us (99%)
    pallas_call x1, Pallas kernels, body(): pl.pallas_call(functools.partial(kernel, nz), out_shape=[jax.ShapeDtypeSt...  98 us

profile of v3, /device:TPU:33, one launch (start us, length us, event | category | flops | bytes accessed | tf_op | source)
XLA Modules:
  0.0 99.7 jit_solution(15635315249224883121)
XLA Ops:
  0.6 98.0 %averaging.1 = (f32[16,24,128]{2,1,0:T(8,128)S(1)}, f32[16,24,128]{2,1,0:T(8,128)S(1)}, f32[1,128]{1,0:T(1,128)S(1)}) custom-call(bf16[80,128]{1,0:T(8,128)(2,1)} %part_hbm.1, bf16[256,128]{1,0:T(8,128)(2,1)} %cls_hbm.1, f32[8,64]{1,0:T(8,128)} %ctf_hbm.1, f32[1,64]{1,0:T(1,128)} %bitcast.5, s32[1,64]{1,0:T(1,128)} %bitcast.6, s32[48,64]{1,0:T(8,128)} %tab_hbm.1, ...), custom_call_target="tpu_custom_call" | custom-call | tf_op jit(solution)/shard_map/averaging/pallas_call | solution.py:707
  98.6 1.1 %finish.1 = (f32[256,128]{1,0:T(8,128)}, f32[64,256]{1,0:T(8,128)}, f32[1,80]{1,0:T(1,128)}) custom-call(f32[16,24,128]{2,1,0:T(8,128)S(1)} %get-tuple-element.9.mine_ref, f32[16,24,128]{2,1,0:T(8,128)S(1)} %get-tuple-element.10.other_ref, f32[1,128]{1,0:T(1,128)S(1)} %get-tuple-element.11.ev_ref), custom_call_target="tpu_custom_call" | custom-call | tf_op jit(solution)/shard_map/finish/pallas_call | solution.py:765

commit v4 on v3

--- a/solution.py
+++ b/solution.py
@@ -13,6 +13,7 @@
 SIDE = 4
 NP = ROW * SIDE
 OWNERS = 4
+KEPT = 3
 LANES = 128
 F32 = jnp.float32
 BF16 = jnp.bfloat16
@@ -111,6 +112,7 @@
     lse_first,
     lse_own,
     lse_all,
+    raw,
     post,
     frame,
     out_send,
@@ -456,8 +458,9 @@
         tell(owner_in.at[2], far(0))
         tell(owner_in.at[3], far(0))
 
+    kept_back = jnp.where(owner < OWNERS, KEPT, 0)
     with jax.named_scope("sources"):
-        each(0, NP // 2, prepare_sources)
+        each(kept_back, NP // 2, prepare_sources)
 
     later = zb >= nb // 2
 
@@ -491,24 +494,21 @@
         top_send[...] = jnp.concatenate([peak, evidence], axis=0)
         lse_send[...] = evidence
 
-        each(
-            0,
-            NP,
-            lambda k: remote(
-                lse_send, lse_first.at[owner * NP + me], ag_ssem, first_rsem, at(lax.rem(k, ROW), k // ROW)
-            ).start(),
-        )
-
-        def send_top(b):
+        for k in range(NP):
+            remote(
+                lse_send, lse_first.at[owner * NP + me], ag_ssem, first_rsem, at(k % ROW, k // ROW)
+            ).start()
+        for b in range(nb):
+
             @pl.when(b != zb)
             def _():
                 remote(top_send, top_recv.at[owner], ag_ssem, top_rsem, far(b)).start()
 
-        each(0, nb, send_top)
         one = (exp_one * 65535.0 + 0.5).astype(jnp.int32)
         two = (exp_two * 65535.0 + 0.5).astype(jnp.int32)
         ag_send[...] = (one & 0xFFFF) | (two << 16)
-
+        with jax.named_scope("kept_back"):
+            each(0, KEPT, prepare_sources)
 
         def send_early(b):
             @pl.when(jnp.logical_not(jnp.logical_and(later, b == 1)))
@@ -542,13 +542,18 @@
             drain(ag_rsem.at[o], ag_send.shape[0])
         remote(ag_recv.at[o], ag_recv.at[o], pass_ssem, ag_rsem.at[o], far(b)).start()
 
+    used = lane((rows, LANES)) < count
+
+    def unpack(o):
+        word = expand(ag_recv[o])
+        raw[rows_of(o, rows), 0:128] = jnp.where(used, (word & 0xFFFF).astype(F32), 0.0)
+        raw[rows_of(o, rows), 128:256] = jnp.where(used, lax.shift_right_logical(word, 16).astype(F32), 0.0)
+
     @pl.when(zb == 0)
     def _():
         for o in range(OWNERS):
             pass_post(o, nb - 1 if o < OWNERS // 2 else 1)
-
-    @pl.when(zb == 0)
-    def _():
+        each(0, OWNERS, unpack)
         with jax.named_scope("first_in"):
             drain(first_rsem, OWNERS * NP)
         ev_ref[...] = merged(lse_first[...], 0)[0]
@@ -564,8 +569,6 @@
         ev_ref[...] = merged(lse_all[...], 0)[0]
 
     evidence = ev_ref[...]
-    used = lane((rows, LANES)) < count
-
     def take_post(o):
         passes = jnp.logical_and(zb == nb - 1, o < OWNERS // 2)
 
@@ -578,12 +581,14 @@
             with jax.named_scope("post_in"):
                 drain(ag_rsem.at[o], ag_send.shape[0])
 
-        word = expand(ag_recv[o])
+        @pl.when(zb > 0)
+        def _():
+            unpack(o)
+
         scale = jnp.exp(top_recv[o, 0:1] - evidence) * (1.0 / 65535.0)
-        one = jnp.where(used, (word & 0xFFFF).astype(F32) * scale, 0.0)
-        two = jnp.where(used, lax.shift_right_logical(word, 16).astype(F32) * scale, 0.0)
-        post[rows_of(o, rows), 0:128] = one.astype(BF16)
-        post[rows_of(o, rows), 128:256] = two.astype(BF16)
+        scale = jnp.where(lane((1, LANES)) < count, scale, 0.0)
+        post[rows_of(o, rows), 0:128] = (raw[rows_of(o, rows), 0:128] * scale).astype(BF16)
+        post[rows_of(o, rows), 128:256] = (raw[rows_of(o, rows), 128:256] * scale).astype(BF16)
 
     each(0, OWNERS, take_post)
 
@@ -737,6 +742,7 @@
             vmem((OWNERS * NP, 1, LANES), F32),
             vmem((1, LANES), F32),
             vmem((NP, 1, LANES), F32),
+            vmem((pairs, 2 * LANES), F32),
             vmem((pairs, 2 * LANES), BF16),
             vmem((ROW // 2, 6 * kb, half * LANES), BF16),
             vmem((NP, 24, LANES), F32),

time: 99.9 us -> 100 us (level)
  no operation moved by 1% of the time
where the time goes in v4:
time: 100 us
  Pallas kernels  99.3 us (99%)
    pallas_call x1, Pallas kernels, body(): pl.pallas_call(functools.partial(kernel, nz), out_shape=[jax.ShapeDtypeSt...  98.2 us

profile of v4, /device:TPU:33, one launch (start us, length us, event | category | flops | bytes accessed | tf_op | source)
XLA Modules:
  0.0 100.0 jit_solution(10338702198055210517)
XLA Ops:
  0.6 98.2 %averaging.1 = (f32[16,24,128]{2,1,0:T(8,128)S(1)}, f32[16,24,128]{2,1,0:T(8,128)S(1)}, f32[1,128]{1,0:T(1,128)S(1)}) custom-call(bf16[80,128]{1,0:T(8,128)(2,1)} %part_hbm.1, bf16[256,128]{1,0:T(8,128)(2,1)} %cls_hbm.1, f32[8,64]{1,0:T(8,128)} %ctf_hbm.1, f32[1,64]{1,0:T(1,128)} %bitcast.5, s32[1,64]{1,0:T(1,128)} %bitcast.6, s32[48,64]{1,0:T(8,128)} %tab_hbm.1, ...), custom_call_target="tpu_custom_call" | custom-call | tf_op jit(solution)/shard_map/averaging/pallas_call | solution.py:712
  98.9 1.1 %finish.1 = (f32[256,128]{1,0:T(8,128)}, f32[64,256]{1,0:T(8,128)}, f32[1,80]{1,0:T(1,128)}) custom-call(f32[16,24,128]{2,1,0:T(8,128)S(1)} %get-tuple-element.9.mine_ref, f32[16,24,128]{2,1,0:T(8,128)S(1)} %get-tuple-element.10.other_ref, f32[1,128]{1,0:T(1,128)S(1)} %get-tuple-element.11.ev_ref), custom_call_target="tpu_custom_call" | custom-call | tf_op jit(solution)/shard_map/finish/pallas_call | solution.py:771

commit v5 on v3

--- a/solution.py
+++ b/solution.py
@@ -615,7 +615,7 @@
                         ),
                     ],
                     axis=0,
-                )
+                ).astype(BF16)
         for k in range(ROW):
             to = lax.rem(x + k, ROW)
             b = i * ROW + to
@@ -627,7 +627,7 @@
     with jax.named_scope("class_rows"):
         each(0, SIDE, class_row)
     mine_ref[me] = out_send[me]
-    out_size = (NP - 1) * out_send.shape[1]
+    out_size = (NP - 1) * out_send.shape[1] // 2
     with jax.named_scope("take_out"):
         drain(o_rsem, out_size)
 
@@ -670,7 +670,7 @@
     coef, kb = cw_ref.shape[0], cs_ref.shape[0] // NP
     halves = []
     for b in range(NP):
-        both = mine_ref[b] + other_ref[b]
+        both = mine_ref[b].astype(F32) + other_ref[b].astype(F32)
         cs_ref[b * kb : (b + 1) * kb, :] = both[:kb]
         halves.append(both[kb:])
     for first in range(0, NP, NP // 2):
@@ -707,8 +707,8 @@
     mine, other, evidence = pl.pallas_call(
         functools.partial(kernel, nz),
         out_shape=[
-            jax.ShapeDtypeStruct((NP, 24, LANES), F32),
-            jax.ShapeDtypeStruct((NP, 24, LANES), F32),
+            jax.ShapeDtypeStruct((NP, 24, LANES), BF16),
+            jax.ShapeDtypeStruct((NP, 24, LANES), BF16),
             jax.ShapeDtypeStruct((1, LANES), F32),
         ],
         in_specs=[pl.BlockSpec(memory_space=pltpu.HBM)] * 7,
@@ -739,7 +739,7 @@
             vmem((NP, 1, LANES), F32),
             vmem((pairs, 2 * LANES), BF16),
             vmem((ROW // 2, 6 * kb, half * LANES), BF16),
-            vmem((NP, 24, LANES), F32),
+            vmem((NP, 24, LANES), BF16),
             vmem((1152, 1, LANES), F32),
             dma((len(arrays) + 1,)),
             dma,

time: 99.9 us -> 99.3 us (level)
  no operation moved by 1% of the time
where the time goes in v5:
time: 99.3 us; the launch traced here: 99.1 us
  Pallas kernels  98.5 us (99%)
    pallas_call x1, Pallas kernels, body(): pl.pallas_call(functools.partial(kernel, nz), out_shape=[jax.ShapeDtypeSt...  97.4 us

profile of v5, /device:TPU:33, one launch (start us, length us, event | category | flops | bytes accessed | tf_op | source)
XLA Modules:
  0.0 99.1 jit_solution(5729577080099062742)
XLA Ops:
  0.6 97.4 %averaging.1 = (bf16[16,24,128]{2,1,0:T(8,128)(2,1)S(1)}, bf16[16,24,128]{2,1,0:T(8,128)(2,1)S(1)}, f32[1,128]{1,0:T(1,128)S(1)}) custom-call(bf16[80,128]{1,0:T(8,128)(2,1)} %part_hbm.1, bf16[256,128]{1,0:T(8,128)(2,1)} %cls_hbm.1, f32[8,64]{1,0:T(8,128)} %ctf_hbm.1, f32[1,64]{1,0:T(1,128)} %bitcast.5, s32[1,64]{1,0:T(1,128)} %bitcast.6, s32[48,64]{1,0:T(8,128)} %tab_hbm.1, ...), custom_call_target="tpu_custom_call" | custom-call | tf_op jit(solution)/shard_map/averaging/pallas_call | solution.py:707
  98.1 1.1 %finish.1 = (f32[256,128]{1,0:T(8,128)}, f32[64,256]{1,0:T(8,128)}, f32[1,80]{1,0:T(1,128)}) custom-call(bf16[16,24,128]{2,1,0:T(8,128)(2,1)S(1)} %get-tuple-element.9.mine_ref, bf16[16,24,128]{2,1,0:T(8,128)(2,1)S(1)} %get-tuple-element.10.other_ref, f32[1,128]{1,0:T(1,128)S(1)} %get-tuple-element.11.ev_ref), custom_call_target="tpu_custom_call" | custom-call | tf_op jit(solution)/shard_map/finish/pallas_call | solution.py:765

commit v6 on v5

--- a/solution.py
+++ b/solution.py
@@ -12,6 +12,7 @@
 ROW = 4
 SIDE = 4
 NP = ROW * SIDE
+OUTWARD = 2, 1, 3
 OWNERS = 4
 LANES = 128
 F32 = jnp.float32
@@ -250,7 +251,7 @@
 
     def across(i):
         b = i * ROW + x
-        for k in range(1, ROW):
+        for k in OUTWARD:
             to = lax.rem(x + k, ROW)
             device = at(to, z)
             remote(bundle.at[b], bundle.at[b], g_ssem, x_rsem.at[i], device).start()
@@ -616,13 +617,14 @@
                     ],
                     axis=0,
                 ).astype(BF16)
-        for k in range(ROW):
-            to = lax.rem(x + k, ROW)
-            b = i * ROW + to
-
-            @pl.when(b != me)
-            def _():
-                remote(out_send.at[b], mine_ref.at[me], o_ssem, o_rsem, at(to, zb * SIDE + i)).start()
+            nearer = jnp.where(lax.rem(x + 2, ROW) == 2 * k + 1, 0, 1)
+            for t in range(2):
+                to = 2 * k + (1 - nearer if t == 0 else nearer)
+                b = i * ROW + to
+
+                @pl.when(b != me)
+                def _():
+                    remote(out_send.at[b], mine_ref.at[me], o_ssem, o_rsem, at(to, zb * SIDE + i)).start()
 
     with jax.named_scope("class_rows"):
         each(0, SIDE, class_row)

time: 99.3 us -> 99 us (level)
  no operation moved by 1% of the time
where the time goes in v6:
time: 99 us; the launch traced here: 98.8 us
  Pallas kernels  98.2 us (99%)
    pallas_call x1, Pallas kernels, body(): pl.pallas_call(functools.partial(kernel, nz), out_shape=[jax.ShapeDtypeSt...  97.1 us

profile of v6, /device:TPU:33, one launch (start us, length us, event | category | flops | bytes accessed | tf_op | source)
XLA Modules:
  0.0 98.8 jit_solution(1597587933210688294)
XLA Ops:
  0.6 97.1 %averaging.1 = (bf16[16,24,128]{2,1,0:T(8,128)(2,1)S(1)}, bf16[16,24,128]{2,1,0:T(8,128)(2,1)S(1)}, f32[1,128]{1,0:T(1,128)S(1)}) custom-call(bf16[80,128]{1,0:T(8,128)(2,1)} %part_hbm.1, bf16[256,128]{1,0:T(8,128)(2,1)} %cls_hbm.1, f32[8,64]{1,0:T(8,128)} %ctf_hbm.1, f32[1,64]{1,0:T(1,128)} %bitcast.5, s32[1,64]{1,0:T(1,128)} %bitcast.6, s32[48,64]{1,0:T(8,128)} %tab_hbm.1, ...), custom_call_target="tpu_custom_call" | custom-call | tf_op jit(solution)/shard_map/averaging/pallas_call | solution.py:709
  97.7 1.1 %finish.1 = (f32[256,128]{1,0:T(8,128)}, f32[64,256]{1,0:T(8,128)}, f32[1,80]{1,0:T(1,128)}) custom-call(bf16[16,24,128]{2,1,0:T(8,128)(2,1)S(1)} %get-tuple-element.9.mine_ref, bf16[16,24,128]{2,1,0:T(8,128)(2,1)S(1)} %get-tuple-element.10.other_ref, f32[1,128]{1,0:T(1,128)S(1)} %get-tuple-element.11.ev_ref), custom_call_target="tpu_custom_call" | custom-call | tf_op jit(solution)/shard_map/finish/pallas_call | solution.py:767

commit v7 on v4

--- a/solution.py
+++ b/solution.py
@@ -12,8 +12,8 @@
 ROW = 4
 SIDE = 4
 NP = ROW * SIDE
+OUTWARD = 2, 1, 3
 OWNERS = 4
-KEPT = 3
 LANES = 128
 F32 = jnp.float32
 BF16 = jnp.bfloat16
@@ -252,7 +252,7 @@
 
     def across(i):
         b = i * ROW + x
-        for k in range(1, ROW):
+        for k in OUTWARD:
             to = lax.rem(x + k, ROW)
             device = at(to, z)
             remote(bundle.at[b], bundle.at[b], g_ssem, x_rsem.at[i], device).start()
@@ -458,9 +458,8 @@
         tell(owner_in.at[2], far(0))
         tell(owner_in.at[3], far(0))
 
-    kept_back = jnp.where(owner < OWNERS, KEPT, 0)
     with jax.named_scope("sources"):
-        each(kept_back, NP // 2, prepare_sources)
+        each(0, NP // 2, prepare_sources)
 
     later = zb >= nb // 2
 
@@ -507,8 +506,7 @@
         one = (exp_one * 65535.0 + 0.5).astype(jnp.int32)
         two = (exp_two * 65535.0 + 0.5).astype(jnp.int32)
         ag_send[...] = (one & 0xFFFF) | (two << 16)
-        with jax.named_scope("kept_back"):
-            each(0, KEPT, prepare_sources)
+
 
         def send_early(b):
             @pl.when(jnp.logical_not(jnp.logical_and(later, b == 1)))
@@ -620,19 +618,20 @@
                         ),
                     ],
                     axis=0,
-                )
-        for k in range(ROW):
-            to = lax.rem(x + k, ROW)
-            b = i * ROW + to
-
-            @pl.when(b != me)
-            def _():
-                remote(out_send.at[b], mine_ref.at[me], o_ssem, o_rsem, at(to, zb * SIDE + i)).start()
+                ).astype(BF16)
+            nearer = jnp.where(lax.rem(x + 2, ROW) == 2 * k + 1, 0, 1)
+            for t in range(2):
+                to = 2 * k + (1 - nearer if t == 0 else nearer)
+                b = i * ROW + to
+
+                @pl.when(b != me)
+                def _():
+                    remote(out_send.at[b], mine_ref.at[me], o_ssem, o_rsem, at(to, zb * SIDE + i)).start()
 
     with jax.named_scope("class_rows"):
         each(0, SIDE, class_row)
     mine_ref[me] = out_send[me]
-    out_size = (NP - 1) * out_send.shape[1]
+    out_size = (NP - 1) * out_send.shape[1] // 2
     with jax.named_scope("take_out"):
         drain(o_rsem, out_size)
 
@@ -675,7 +674,7 @@
     coef, kb = cw_ref.shape[0], cs_ref.shape[0] // NP
     halves = []
     for b in range(NP):
-        both = mine_ref[b] + other_ref[b]
+        both = mine_ref[b].astype(F32) + other_ref[b].astype(F32)
         cs_ref[b * kb : (b + 1) * kb, :] = both[:kb]
         halves.append(both[kb:])
     for first in range(0, NP, NP // 2):
@@ -712,8 +711,8 @@
     mine, other, evidence = pl.pallas_call(
         functools.partial(kernel, nz),
         out_shape=[
-            jax.ShapeDtypeStruct((NP, 24, LANES), F32),
-            jax.ShapeDtypeStruct((NP, 24, LANES), F32),
+            jax.ShapeDtypeStruct((NP, 24, LANES), BF16),
+            jax.ShapeDtypeStruct((NP, 24, LANES), BF16),
             jax.ShapeDtypeStruct((1, LANES), F32),
         ],
         in_specs=[pl.BlockSpec(memory_space=pltpu.HBM)] * 7,
@@ -745,7 +744,7 @@
             vmem((pairs, 2 * LANES), F32),
             vmem((pairs, 2 * LANES), BF16),
             vmem((ROW // 2, 6 * kb, half * LANES), BF16),
-            vmem((NP, 24, LANES), F32),
+            vmem((NP, 24, LANES), BF16),
             vmem((1152, 1, LANES), F32),
             dma((len(arrays) + 1,)),
             dma,

time: 100 us -> 98.6 us (0.986)
  Pallas kernels: 99.3 us -> 97.7 us
    pallas_call x1, Pallas kernels: 98.2 us -> 96.7 us  [body(): pl.pallas_call(functools.partial(kernel, nz), out_shape=[jax.ShapeDtypeSt...]
where the time goes in v7:
time: 98.6 us; the launch traced here: 98.4 us
  Pallas kernels  97.7 us (99%)
    pallas_call x1, Pallas kernels, body(): pl.pallas_call(functools.partial(kernel, nz), out_shape=[jax.ShapeDtypeSt...  96.7 us

profile of v7, /device:TPU:33, one launch (start us, length us, event | category | flops | bytes accessed | tf_op | source)
XLA Modules:
  0.0 98.4 jit_solution(3862230186793760057)
XLA Ops:
  0.6 96.7 %averaging.1 = (bf16[16,24,128]{2,1,0:T(8,128)(2,1)S(1)}, bf16[16,24,128]{2,1,0:T(8,128)(2,1)S(1)}, f32[1,128]{1,0:T(1,128)S(1)}) custom-call(bf16[80,128]{1,0:T(8,128)(2,1)} %part_hbm.1, bf16[256,128]{1,0:T(8,128)(2,1)} %cls_hbm.1, f32[8,64]{1,0:T(8,128)} %ctf_hbm.1, f32[1,64]{1,0:T(1,128)} %bitcast.5, s32[1,64]{1,0:T(1,128)} %bitcast.6, s32[48,64]{1,0:T(8,128)} %tab_hbm.1, ...), custom_call_target="tpu_custom_call" | custom-call | tf_op jit(solution)/shard_map/averaging/pallas_call | solution.py:711
  97.3 1.1 %finish.1 = (f32[256,128]{1,0:T(8,128)}, f32[64,256]{1,0:T(8,128)}, f32[1,80]{1,0:T(1,128)}) custom-call(bf16[16,24,128]{2,1,0:T(8,128)(2,1)S(1)} %get-tuple-element.9.mine_ref, bf16[16,24,128]{2,1,0:T(8,128)(2,1)S(1)} %get-tuple-element.10.other_ref, f32[1,128]{1,0:T(1,128)S(1)} %get-tuple-element.11.ev_ref), custom_call_target="tpu_custom_call" | custom-call | tf_op jit(solution)/shard_map/finish/pallas_call | solution.py:770

commit v8 on v7

--- a/solution.py
+++ b/solution.py
@@ -494,8 +494,9 @@
         lse_send[...] = evidence
 
         for k in range(NP):
+            row = jnp.where(later, SIDE - 1 - k // ROW, k // ROW)
             remote(
-                lse_send, lse_first.at[owner * NP + me], ag_ssem, first_rsem, at(k % ROW, k // ROW)
+                lse_send, lse_first.at[owner * NP + me], ag_ssem, first_rsem, at(k % ROW, row)
             ).start()
         for b in range(nb):
 
@@ -588,7 +589,8 @@
         post[rows_of(o, rows), 0:128] = (raw[rows_of(o, rows), 0:128] * scale).astype(BF16)
         post[rows_of(o, rows), 128:256] = (raw[rows_of(o, rows), 128:256] * scale).astype(BF16)
 
-    each(0, OWNERS, take_post)
+    for o in range(OWNERS):
+        take_post(o)
 
     def class_row(i):
         pairs_in = [i * (ROW // 2) + k for k in range(ROW // 2)]

time: 98.6 us -> 98.3 us (level)
  no operation moved by 1% of the time
where the time goes in v8:
time: 98.3 us; the launch traced here: 98.1 us
  Pallas kernels  97.5 us (99%)
    pallas_call x1, Pallas kernels, body(): pl.pallas_call(functools.partial(kernel, nz), out_shape=[jax.ShapeDtypeSt...  96.4 us

profile of v8, /device:TPU:33, one launch (start us, length us, event | category | flops | bytes accessed | tf_op | source)
XLA Modules:
  0.0 98.1 jit_solution(15542991323241559141)
XLA Ops:
  0.6 96.4 %averaging.1 = (bf16[16,24,128]{2,1,0:T(8,128)(2,1)S(1)}, bf16[16,24,128]{2,1,0:T(8,128)(2,1)S(1)}, f32[1,128]{1,0:T(1,128)S(1)}) custom-call(bf16[80,128]{1,0:T(8,128)(2,1)} %part_hbm.1, bf16[256,128]{1,0:T(8,128)(2,1)} %cls_hbm.1, f32[8,64]{1,0:T(8,128)} %ctf_hbm.1, f32[1,64]{1,0:T(1,128)} %bitcast.5, s32[1,64]{1,0:T(1,128)} %bitcast.6, s32[48,64]{1,0:T(8,128)} %tab_hbm.1, ...), custom_call_target="tpu_custom_call" | custom-call | tf_op jit(solution)/shard_map/averaging/pallas_call | solution.py:713
  97.1 1.1 %finish.1 = (f32[256,128]{1,0:T(8,128)}, f32[64,256]{1,0:T(8,128)}, f32[1,80]{1,0:T(1,128)}) custom-call(bf16[16,24,128]{2,1,0:T(8,128)(2,1)S(1)} %get-tuple-element.9.mine_ref, bf16[16,24,128]{2,1,0:T(8,128)(2,1)S(1)} %get-tuple-element.10.other_ref, f32[1,128]{1,0:T(1,128)S(1)} %get-tuple-element.11.ev_ref), custom_call_target="tpu_custom_call" | custom-call | tf_op jit(solution)/shard_map/finish/pallas_call | solution.py:772
